TPU v7x, 512 devices: a 4x2x32 block of a 4x8x32 slice. The times are simulated.
512 devices in a mesh: scen: 2 (over y), row: 32 (over z), col: 4 (over x), layer: 2 (over core).
Axes of the slice: x: 4, y: 2, z: 32, core: 2. Of those that a mesh axis runs over, the one named last changes fastest.
The devices are a block of a 4x8x32 slice.
Arguments:
- current: float32 [2, 8192, 4096], P('layer', ('scen', 'row'), 'col'), parts along dimension 1, may hold values from 0.5 to 10
- node_class: int32 [2, 8192, 4096], P('layer', ('scen', 'row'), 'col'), parts along dimension 1, may hold values from 0 to 7
- class_conductance: float32 [2, 8], P('layer'), may hold values from 0.5 to 4
- pad_mask: int32 [2, 8192, 4096], P('layer', ('scen', 'row'), 'col'), parts along dimension 1, may hold values 0 or 1
- via_mask: int32 [8192, 4096], P(('scen', 'row'), 'col'), parts along dimension 0, may hold values 0 or 1
Outputs:
- drop: float32 [2, 8192, 4096], P('layer', ('scen', 'row'), 'col'), parts along dimension 1
- residual: float32 [2, 8192, 4096], P('layer', ('scen', 'row'), 'col'), parts along dimension 1
- worst: float32 [2, 8192, 4096], P('layer', ('scen', 'row'), 'col'), parts along dimension 1
There are 2 independent parts, one for each index of `scen`. A program takes and returns all parts, laid end to end along the dimension named above; an argument that names none is the same for every part. Nothing has to cross between parts.
All inputs are finite; a program needn't handle non-finite values. No bound on the sum of `pad_mask` or of `via_mask` on one device may be relied on, other than what follows from the above.
Results may differ from a plain program's by a relative error of at most 0.0003.
Values sent between devices are 32-bit elements; how exact they have to be, the bound alone decides.
No kernel may reach another device: no remote copies, remote signals or barrier semaphores. Data moves between devices by JAX's collectives and lax.ppermute only.
A program may use at most 64 MiB of HBM per device.

v0:
```python
import functools

import jax
import jax.numpy as jnp
from jax import lax
from jax.sharding import PartitionSpec as P

ITERS = 2


via_conductance = 2.0
pad_conductance = 4.0
leakage = 0.05


def with_halo(value, sides, width):
    edges = {}
    for axis, dim in sides:
        size, length = (lax.axis_size(axis), value.shape[dim])
        up = [(i, (i + 1) % size) for i in range(size - 1)]
        last = lax.slice_in_dim(value, length - width, length, axis=dim)
        initial = lax.slice_in_dim(value, 0, width, axis=dim)
        edges[dim] = (
            lax.ppermute(last, axis, up),
            lax.ppermute(initial, axis, [(b, a) for a, b in up]),
        )
    done = []
    for _, dim in sides:
        low, high = edges[dim]
        around = [(width, width) if d in done else (0, 0) for d in range(value.ndim)]
        value = jnp.concatenate([jnp.pad(low, around), value, jnp.pad(high, around)], axis=dim)
        done.append(dim)
    return value


def from_partner(value, axis, stride):
    return lax.ppermute(value, axis, [(i, i ^ 1 << stride) for i in range(lax.axis_size(axis))])


def over_axes(value, axes):
    return functools.reduce(lax.psum, axes, value)


def lookup(node_class, class_conductance):
    cond = jnp.zeros(node_class.shape, jnp.float32)
    for klass in range(class_conductance.shape[1]):
        cond = cond + jnp.where(
            node_class == klass, class_conductance[:, klass][:, None, None], jnp.float32(0.0)
        )
    return cond


def edge_terms(cond):
    padded = with_halo(cond, (("row", 1), ("col", 2)), 1)
    beside_all = (
        padded[:, :-2, 1:-1],
        padded[:, 2:, 1:-1],
        padded[:, 1:-1, :-2],
        padded[:, 1:-1, 2:],
    )
    return tuple(
        (jnp.where(other > 0.0, 0.5 * (cond + other), jnp.float32(0.0)) for other in beside_all)
    )


def apply_grid(values, edges, diagonal, coupling):
    padded = with_halo(values, (("row", 1), ("col", 2)), 1)
    partner = from_partner(values, "layer", 0)
    beside = edges[0] * padded[:, :-2, 1:-1] + edges[1] * padded[:, 2:, 1:-1]
    beside = beside + edges[2] * padded[:, 1:-1, :-2] + edges[3] * padded[:, 1:-1, 2:]
    return diagonal * values - beside - coupling * partner


def local(current, node_class, class_conductance, pad_mask, via_mask):
    cond = lookup(node_class, class_conductance)
    edges = edge_terms(cond)
    coupling = via_conductance * via_mask.astype(jnp.float32)
    diagonal = (
        edges[0]
        + edges[1]
        + edges[2]
        + edges[3]
        + coupling
        + pad_conductance * pad_mask.astype(jnp.float32)
        + leakage
    )
    drop_field = jnp.zeros_like(current)
    resid = current
    worst_field = drop_field

    def inner_pair(resid_now):
        precond_now = resid_now / diagonal
        image_now = apply_grid(precond_now, edges, diagonal, coupling)
        energy_part, curve_part = (
            over_axes(jnp.sum(resid_now * precond_now), ("row", "col", "layer")),
            over_axes(jnp.sum(precond_now * image_now), ("row", "col", "layer")),
        )
        return (precond_now, image_now, energy_part, curve_part)

    precond, image, energy_now, curve_now = inner_pair(resid)
    step_size = energy_now / curve_now
    direction, along = (precond, image)
    for iteration in range(ITERS):
        drop_field = drop_field + step_size * direction
        resid = resid - step_size * along
        worst_field = drop_field if iteration == 0 else jnp.maximum(worst_field, drop_field)
        if iteration + 1 < ITERS:
            precond, image, energy_next, curve_now = inner_pair(resid)
            ratio = energy_next / energy_now
            step_size = energy_next / (curve_now - ratio * energy_next / step_size)
            direction = precond + ratio * direction
            along = image + ratio * along
            energy_now = energy_next
    return (drop_field, resid, worst_field)


def solution(mesh):
    in_specs = (
        P("layer", ("scen", "row"), "col"),
        P("layer", ("scen", "row"), "col"),
        P("layer", None),
        P("layer", ("scen", "row"), "col"),
        P(("scen", "row"), "col"),
    )
    out_specs = (
        P("layer", ("scen", "row"), "col"),
        P("layer", ("scen", "row"), "col"),
        P("layer", ("scen", "row"), "col"),
    )
    return jax.shard_map(local, mesh=mesh, in_specs=in_specs, out_specs=out_specs, check_vma=False)
```

profile of v0, /device:TPU:33, one launch (start us, length us, event | category | flops | bytes accessed | tf_op | source)
XLA Modules:
  0.0 248.5 jit_solution(104000323186430484)
XLA Ops:
  0.6 1.6 fusion.45
  2.3 6.6 %select_add_fusion = f32[1,128,1024]{2,1,0:T(8,128)S(1)} fusion(s32[1,128,1024]{2,1,0:T(8,128)} %param.6, f32[]{:T(128)} %bitcast.7, f32[]{:T(128)} %bitcast.6, f32[]{:T(128)} %bitcast.5, f32[]{:T(128)} %bitcast.4, f32[]{:T(128)} %bitcast.3, f32[]{:T(128)} %bitcast.2, f32[]{:T(128)} %bitcast.1, f32[]{:T(128)} %bitcast), kind=kLoop, calls=%fused_computation.73 | loop fusion | flops 3014656 | bytes 1048608 | tf_op jit(solution)/shard_map/add | solution.py:47
  8.8 5.2 %collective-permute-start = (f32[1,1,1024]{2,1,0:T(1,128)S(1)}, f32[1,1,1024]{2,1,0:T(1,128)S(1)}, u32[]{:S(2)}, u32[]{:S(2)}) collective-permute-start(f32[1,1,1024]{2,1,0:T(1,128)S(1)} %get-tuple-element.35), channel_id=1, source_target_pairs={{0,8},{8,16},{16,24},{24,32},{32,40},{40,48},{48,56},{56,64},{64,7... | collective-permute-start | bytes 12296 | tf_op jit(solution)/shard_map/ppermute | solution.py:24
  14.1 1.3 collective-permute-start.1
  15.4 0.1 fusion.43
  15.5 3.3 %collective-permute-start.2 = (f32[1,128,1]{2,1,0:T(8,128)S(1)}, f32[1,128,1]{2,1,0:T(8,128)S(1)}, u32[]{:S(2)}, u32[]{:S(2)}) collective-permute-start(f32[1,128,1]{2,1,0:T(8,128)S(1)} %get-tuple-element.33), channel_id=1, source_target_pairs={{0,2},{2,4},{4,6},{1,3},{3,5},{5,7},{8,10},{10,12},{12,14},{9,11},... | collective-permute-start | bytes 1544 | tf_op jit(solution)/shard_map/ppermute | solution.py:24
  18.8 1.3 collective-permute-start.3
  20.1 0.0 collective-permute-done.2
  20.1 3.7 %collective-permute-done.3 = f32[1,128,1]{2,1,0:T(8,128)S(1)} collective-permute-done((f32[1,128,1]{2,1,0:T(8,128)S(1)}, f32[1,128,1]{2,1,0:T(8,128)S(1)}, u32[]{:S(2)}, u32[]{:S(2)}) %collective-permute-start.3) | collective-permute-done | bytes 544 | tf_op jit(solution)/shard_map/ppermute | solution.py:25
  23.8 0.0 collective-permute-done
  23.8 0.0 collective-permute-done.1
  23.8 0.0 copy-done
  23.8 0.0 copy-done.1
  23.8 1.7 fusion.37
  25.5 38.6 %collective-permute-start.8 = (f32[1,128,1024]{2,1,0:T(8,128)S(1)}, f32[1,128,1024]{2,1,0:T(8,128)S(1)}, u32[]{:S(2)}, u32[]{:S(2)}) collective-permute-start(f32[1,128,1024]{2,1,0:T(8,128)S(1)} %get-tuple-element.23), channel_id=1, source_target_pairs={{0,1},{1,0},{2,3},{3,2},{4,5},{5,4},{6,7},{7,6},{8,9},{9,8},{10,11... | collective-permute-start | bytes 1572872 | tf_op jit(solution)/shard_map/ppermute | solution.py:37
  64.1 4.3 %collective-permute-start.4 = (f32[1,1,1024]{2,1,0:T(1,128)S(1)}, f32[1,1,1024]{2,1,0:T(1,128)S(1)}, u32[]{:S(2)}, u32[]{:S(2)}) collective-permute-start(f32[1,1,1024]{2,1,0:T(1,128)S(1)} %get-tuple-element.31), channel_id=1, source_target_pairs={{0,8},{8,16},{16,24},{24,32},{32,40},{40,48},{48,56},{56,64},{64,7... | collective-permute-start | bytes 12296 | tf_op jit(solution)/shard_map/ppermute | solution.py:24
  68.5 1.3 collective-permute-start.5
  69.8 0.1 fusion.41
  69.9 1.3 collective-permute-start.6
  71.2 1.3 collective-permute-start.7
  72.5 0.0 collective-permute-done.6
  72.5 3.7 %collective-permute-done.7 = f32[1,128,1]{2,1,0:T(8,128)S(1)} collective-permute-done((f32[1,128,1]{2,1,0:T(8,128)S(1)}, f32[1,128,1]{2,1,0:T(8,128)S(1)}, u32[]{:S(2)}, u32[]{:S(2)}) %collective-permute-start.7) | collective-permute-done | bytes 544 | tf_op jit(solution)/shard_map/ppermute | solution.py:25
  76.2 0.0 collective-permute-done.4
  76.2 0.0 collective-permute-done.5
  76.2 0.0 collective-permute-done.8
  76.2 1.5 multiply_reduce_fusion.2
  77.7 49.8 %all-reduce.7 = (f32[]{:T(128)}, f32[]{:T(128)}) all-reduce(f32[]{:T(128)} %get-tuple-element.6, f32[]{:T(128)} %get-tuple-element.5), channel_id=1, replica_groups=mesh['scen'=2,'row'=32,'col'=4,'layer'=2] {'row'}, use_global_device_ids=true, to_apply=%region_1.2 | all-reduce | flops 2 | bytes 16 | tf_op jit(solution)/shard_map/psum | solution.py:41
  127.5 7.7 %all-reduce.9 = (f32[]{:T(128)}, f32[]{:T(128)}) all-reduce(f32[]{:T(128)} %get-tuple-element.9, f32[]{:T(128)} %get-tuple-element.10), channel_id=1, replica_groups=mesh['scen'=2,'row'=32,'col'=4,'layer'=2] {'col'}, use_global_device_ids=true, to_apply=%region_2.3 | all-reduce | flops 2 | bytes 16 | tf_op jit(solution)/shard_map/psum | solution.py:41
  135.2 21.0 %all-reduce.11 = (f32[]{:T(128)}, f32[]{:T(128)}) all-reduce(f32[]{:T(128)} %get-tuple-element.13, f32[]{:T(128)} %get-tuple-element.14), channel_id=1, replica_groups=mesh['scen'=2,'row'=32,'col'=4,'layer'=2] {'layer'}, use_global_device_ids=true, to_apply=%region_3.4 | all-reduce | flops 2 | bytes 16 | tf_op jit(solution)/shard_map/psum | solution.py:41
  157.5 0.0 copy-start.2
  157.5 0.1 fusion.34
  157.7 2.3 collective-permute-start.13
  160.0 1.3 collective-permute-start.9
  161.3 1.3 collective-permute-start.10
  162.6 0.1 fusion.39
  162.7 2.3 collective-permute-start.11
  165.0 1.3 collective-permute-start.12
  166.4 0.0 collective-permute-done.11
  166.4 3.7 %collective-permute-done.12 = f32[1,128,1]{2,1,0:T(8,128)S(1)} collective-permute-done((f32[1,128,1]{2,1,0:T(8,128)S(1)}, f32[1,128,1]{2,1,0:T(8,128)S(1)}, u32[]{:S(2)}, u32[]{:S(2)}) %collective-permute-start.12) | collective-permute-done | bytes 544 | tf_op jit(solution)/shard_map/ppermute | solution.py:25
  170.1 0.0 collective-permute-done.9
  170.1 0.0 collective-permute-done.10
  170.1 0.0 collective-permute-done.13
  170.1 0.0 copy-done.2
  170.1 2.4 multiply_reduce_fusion
  172.5 41.7 %all-reduce.6 = (f32[]{:T(128)}, f32[]{:T(128)}) all-reduce(f32[]{:T(128)} %get-tuple-element.4, f32[]{:T(128)} %get-tuple-element.3), channel_id=1, replica_groups=mesh['scen'=2,'row'=32,'col'=4,'layer'=2] {'row'}, use_global_device_ids=true, to_apply=%region_9.10 | all-reduce | flops 2 | bytes 16 | tf_op jit(solution)/shard_map/psum | solution.py:41
  214.1 6.7 %all-reduce.8 = (f32[]{:T(128)}, f32[]{:T(128)}) all-reduce(f32[]{:T(128)} %get-tuple-element.7, f32[]{:T(128)} %get-tuple-element.8), channel_id=1, replica_groups=mesh['scen'=2,'row'=32,'col'=4,'layer'=2] {'col'}, use_global_device_ids=true, to_apply=%region_10.11 | all-reduce | flops 2 | bytes 16 | tf_op jit(solution)/shard_map/psum | solution.py:41
  220.9 20.9 %all-reduce.10 = (f32[]{:T(128)}, f32[]{:T(128)}) all-reduce(f32[]{:T(128)} %get-tuple-element.11, f32[]{:T(128)} %get-tuple-element.12), channel_id=1, replica_groups=mesh['scen'=2,'row'=32,'col'=4,'layer'=2] {'layer'}, use_global_device_ids=true, to_apply=%region_11.12 | all-reduce | flops 2 | bytes 16 | tf_op jit(solution)/shard_map/psum | solution.py:41
  246.2 2.3 multiply_maximum_fusion
  (5 shorter events, 0.0 us)
Async XLA Ops:
  2.3 21.6 %copy-start = (f32[1,128,1024]{2,1,0:T(8,128)S(1)}, f32[1,128,1024]{2,1,0:T(8,128)}, u32[]{:S(2)}) copy-start(f32[1,128,1024]{2,1,0:T(8,128)} %param.5) | copy-start | bytes 1572868
  2.3 21.6 %copy-start.1 = (s32[128,1024]{1,0:T(8,128)S(1)}, s32[128,1024]{1,0:T(8,128)}, u32[]{:S(2)}) copy-start(s32[128,1024]{1,0:T(8,128)} %param.9) | copy-start | bytes 1572868
  8.8 15.0 %collective-permute-start = (f32[1,1,1024]{2,1,0:T(1,128)S(1)}, f32[1,1,1024]{2,1,0:T(1,128)S(1)}, u32[]{:S(2)}, u32[]{:S(2)}) collective-permute-start(f32[1,1,1024]{2,1,0:T(1,128)S(1)} %get-tuple-element.35), channel_id=1, source_target_pairs={{0,8},{8,16},{16,24},{24,32},{32,40},{40,48},{48,56},{56,64},{64,7... | collective-permute-start | bytes 12296 | tf_op jit(solution)/shard_map/ppermute | solution.py:24
  14.1 9.7 %collective-permute-start.1 = (f32[1,1,1024]{2,1,0:T(1,128)S(1)}, f32[1,1,1024]{2,1,0:T(1,128)S(1)}, u32[]{:S(2)}, u32[]{:S(2)}) collective-permute-start(f32[1,1,1024]{2,1,0:T(1,128)S(1)} %get-tuple-element.36), channel_id=1, source_target_pairs={{8,0},{16,8},{24,16},{32,24},{40,32},{48,40},{56,48},{64,56},{72,6... | collective-permute-start | bytes 12296 | tf_op jit(solution)/shard_map/ppermute | solution.py:25
  15.5 4.6 %collective-permute-start.2 = (f32[1,128,1]{2,1,0:T(8,128)S(1)}, f32[1,128,1]{2,1,0:T(8,128)S(1)}, u32[]{:S(2)}, u32[]{:S(2)}) collective-permute-start(f32[1,128,1]{2,1,0:T(8,128)S(1)} %get-tuple-element.33), channel_id=1, source_target_pairs={{0,2},{2,4},{4,6},{1,3},{3,5},{5,7},{8,10},{10,12},{12,14},{9,11},... | collective-permute-start | bytes 1544 | tf_op jit(solution)/shard_map/ppermute | solution.py:24
  18.8 5.0 %collective-permute-start.3 = (f32[1,128,1]{2,1,0:T(8,128)S(1)}, f32[1,128,1]{2,1,0:T(8,128)S(1)}, u32[]{:S(2)}, u32[]{:S(2)}) collective-permute-start(f32[1,128,1]{2,1,0:T(8,128)S(1)} %get-tuple-element.34), channel_id=1, source_target_pairs={{2,0},{4,2},{6,4},{3,1},{5,3},{7,5},{10,8},{12,10},{14,12},{11,9},... | collective-permute-start | bytes 1544 | tf_op jit(solution)/shard_map/ppermute | solution.py:25
  25.5 50.7 %collective-permute-start.8 = (f32[1,128,1024]{2,1,0:T(8,128)S(1)}, f32[1,128,1024]{2,1,0:T(8,128)S(1)}, u32[]{:S(2)}, u32[]{:S(2)}) collective-permute-start(f32[1,128,1024]{2,1,0:T(8,128)S(1)} %get-tuple-element.23), channel_id=1, source_target_pairs={{0,1},{1,0},{2,3},{3,2},{4,5},{5,4},{6,7},{7,6},{8,9},{9,8},{10,11... | collective-permute-start | bytes 1572872 | tf_op jit(solution)/shard_map/ppermute | solution.py:37
  64.1 12.1 %collective-permute-start.4 = (f32[1,1,1024]{2,1,0:T(1,128)S(1)}, f32[1,1,1024]{2,1,0:T(1,128)S(1)}, u32[]{:S(2)}, u32[]{:S(2)}) collective-permute-start(f32[1,1,1024]{2,1,0:T(1,128)S(1)} %get-tuple-element.31), channel_id=1, source_target_pairs={{0,8},{8,16},{16,24},{24,32},{32,40},{40,48},{48,56},{56,64},{64,7... | collective-permute-start | bytes 12296 | tf_op jit(solution)/shard_map/ppermute | solution.py:24
  68.5 7.8 %collective-permute-start.5 = (f32[1,1,1024]{2,1,0:T(1,128)S(1)}, f32[1,1,1024]{2,1,0:T(1,128)S(1)}, u32[]{:S(2)}, u32[]{:S(2)}) collective-permute-start(f32[1,1,1024]{2,1,0:T(1,128)S(1)} %get-tuple-element.32), channel_id=1, source_target_pairs={{8,0},{16,8},{24,16},{32,24},{40,32},{48,40},{56,48},{64,56},{72,6... | collective-permute-start | bytes 12296 | tf_op jit(solution)/shard_map/ppermute | solution.py:25
  69.9 2.6 %collective-permute-start.6 = (f32[1,128,1]{2,1,0:T(8,128)S(1)}, f32[1,128,1]{2,1,0:T(8,128)S(1)}, u32[]{:S(2)}, u32[]{:S(2)}) collective-permute-start(f32[1,128,1]{2,1,0:T(8,128)S(1)} %get-tuple-element.29), channel_id=1, source_target_pairs={{0,2},{2,4},{4,6},{1,3},{3,5},{5,7},{8,10},{10,12},{12,14},{9,11},... | collective-permute-start | bytes 1544 | tf_op jit(solution)/shard_map/ppermute | solution.py:24
  71.2 5.0 %collective-permute-start.7 = (f32[1,128,1]{2,1,0:T(8,128)S(1)}, f32[1,128,1]{2,1,0:T(8,128)S(1)}, u32[]{:S(2)}, u32[]{:S(2)}) collective-permute-start(f32[1,128,1]{2,1,0:T(8,128)S(1)} %get-tuple-element.30), channel_id=1, source_target_pairs={{2,0},{4,2},{6,4},{3,1},{5,3},{7,5},{10,8},{12,10},{14,12},{11,9},... | collective-permute-start | bytes 1544 | tf_op jit(solution)/shard_map/ppermute | solution.py:25
  157.5 12.6 %copy-start.2 = (s32[128,1024]{1,0:T(8,128)S(1)}, s32[128,1024]{1,0:T(8,128)}, u32[]{:S(2)}) copy-start(s32[128,1024]{1,0:T(8,128)} %param.9) | copy-start | bytes 1572868
  157.7 12.4 %collective-permute-start.13 = (f32[1,128,1024]{2,1,0:T(8,128)S(1)}, f32[1,128,1024]{2,1,0:T(8,128)S(1)}, u32[]{:S(2)}, u32[]{:S(2)}) collective-permute-start(f32[1,128,1024]{2,1,0:T(8,128)S(1)} %fusion.34), channel_id=1, source_target_pairs={{0,1},{1,0},{2,3},{3,2},{4,5},{5,4},{6,7},{7,6},{8,9},{9,8},{10,11... | collective-permute-start | bytes 1572872 | tf_op jit(solution)/shard_map/ppermute | solution.py:37
  160.0 10.1 %collective-permute-start.9 = (f32[1,1,1024]{2,1,0:T(1,128)S(1)}, f32[1,1,1024]{2,1,0:T(1,128)S(1)}, u32[]{:S(2)}, u32[]{:S(2)}) collective-permute-start(f32[1,1,1024]{2,1,0:T(1,128)S(1)} %get-tuple-element.27), channel_id=1, source_target_pairs={{0,8},{8,16},{16,24},{24,32},{32,40},{40,48},{48,56},{56,64},{64,7... | collective-permute-start | bytes 12296 | tf_op jit(solution)/shard_map/ppermute | solution.py:24
  161.3 8.8 %collective-permute-start.10 = (f32[1,1,1024]{2,1,0:T(1,128)S(1)}, f32[1,1,1024]{2,1,0:T(1,128)S(1)}, u32[]{:S(2)}, u32[]{:S(2)}) collective-permute-start(f32[1,1,1024]{2,1,0:T(1,128)S(1)} %get-tuple-element.28), channel_id=1, source_target_pairs={{8,0},{16,8},{24,16},{32,24},{40,32},{48,40},{56,48},{64,56},{72,6... | collective-permute-start | bytes 12296 | tf_op jit(solution)/shard_map/ppermute | solution.py:25
  162.7 3.7 %collective-permute-start.11 = (f32[1,128,1]{2,1,0:T(8,128)S(1)}, f32[1,128,1]{2,1,0:T(8,128)S(1)}, u32[]{:S(2)}, u32[]{:S(2)}) collective-permute-start(f32[1,128,1]{2,1,0:T(8,128)S(1)} %get-tuple-element.25), channel_id=1, source_target_pairs={{0,2},{2,4},{4,6},{1,3},{3,5},{5,7},{8,10},{10,12},{12,14},{9,11},... | collective-permute-start | bytes 1544 | tf_op jit(solution)/shard_map/ppermute | solution.py:24
  165.0 5.0 %collective-permute-start.12 = (f32[1,128,1]{2,1,0:T(8,128)S(1)}, f32[1,128,1]{2,1,0:T(8,128)S(1)}, u32[]{:S(2)}, u32[]{:S(2)}) collective-permute-start(f32[1,128,1]{2,1,0:T(8,128)S(1)} %get-tuple-element.26), channel_id=1, source_target_pairs={{2,0},{4,2},{6,4},{3,1},{5,3},{7,5},{10,8},{12,10},{14,12},{11,9},... | collective-permute-start | bytes 1544 | tf_op jit(solution)/shard_map/ppermute | solution.py:25
where the time goes:
time: 249 us
  blocking collectives  148 us (59%)
  starting transfers between devices  66.5 us (27%)
  other arithmetic  14.5 us (6%)
  waiting for transfers between devices  11.2 us (4%)
  between operations  6.62 us (3%)
    psum x6, blocking collectives, over_axes(): return functools.reduce(lax.psum, axes, value)  148 us
    ppermute x2, starting transfers between devices, from_partner(): lax.ppermute(value, axis, [(i, i ^ 1 << stride) for i in range(lax.axis_s...  40.9 us
    ppermute x6, starting transfers between devices, with_halo(): lax.ppermute(last, axis, up)  17.8 us
    ppermute x6, waiting for transfers between devices, with_halo(): lax.ppermute(initial, axis, [(b, a) for a, b in up])  11.2 us
    ppermute x6, starting transfers between devices, with_halo(): lax.ppermute(initial, axis, [(b, a) for a, b in up])  7.85 us
    add x1, other arithmetic, lookup(): cond + jnp.where(node_class == klass, class_conductance[:, klass][:, None...  6.57 us
  transfers between devices with their start and end apart: 14, of which 3 were waited for; matrix products, arithmetic and copies ran while one was open for 0% of the time, Pallas kernels for 0%

commit v1 on v0

--- a/solution.py
+++ b/solution.py
@@ -1,12 +1,7 @@
-import functools
-
 import jax
 import jax.numpy as jnp
 from jax import lax
 from jax.sharding import PartitionSpec as P
-
-ITERS = 2
-
 
 via_conductance = 2.0
 pad_conductance = 4.0
@@ -37,8 +32,14 @@
     return lax.ppermute(value, axis, [(i, i ^ 1 << stride) for i in range(lax.axis_size(axis))])
 
 
-def over_axes(value, axes):
-    return functools.reduce(lax.psum, axes, value)
+def global_sums(fields):
+    axes = ("row", "col", "layer")
+    count = 1
+    for axis in axes:
+        count *= lax.axis_size(axis)
+    parts = jnp.stack([jnp.sum(field) for field in fields])
+    sent = jnp.broadcast_to(parts[None, None, :], (count, 1, parts.shape[0]))
+    return jnp.sum(lax.all_to_all(sent, axes, 0, 0, tiled=True), axis=(0, 1))
 
 
 def lookup(node_class, class_conductance):
@@ -84,34 +85,25 @@
         + pad_conductance * pad_mask.astype(jnp.float32)
         + leakage
     )
-    drop_field = jnp.zeros_like(current)
-    resid = current
-    worst_field = drop_field
-
-    def inner_pair(resid_now):
-        precond_now = resid_now / diagonal
-        image_now = apply_grid(precond_now, edges, diagonal, coupling)
-        energy_part, curve_part = (
-            over_axes(jnp.sum(resid_now * precond_now), ("row", "col", "layer")),
-            over_axes(jnp.sum(precond_now * image_now), ("row", "col", "layer")),
-        )
-        return (precond_now, image_now, energy_part, curve_part)
-
-    precond, image, energy_now, curve_now = inner_pair(resid)
-    step_size = energy_now / curve_now
-    direction, along = (precond, image)
-    for iteration in range(ITERS):
-        drop_field = drop_field + step_size * direction
-        resid = resid - step_size * along
-        worst_field = drop_field if iteration == 0 else jnp.maximum(worst_field, drop_field)
-        if iteration + 1 < ITERS:
-            precond, image, energy_next, curve_now = inner_pair(resid)
-            ratio = energy_next / energy_now
-            step_size = energy_next / (curve_now - ratio * energy_next / step_size)
-            direction = precond + ratio * direction
-            along = image + ratio * along
-            energy_now = energy_next
-    return (drop_field, resid, worst_field)
+    scaled = current / diagonal
+    image = apply_grid(scaled, edges, diagonal, coupling)
+    second = image / diagonal
+    second_image = apply_grid(second, edges, diagonal, coupling)
+    sums = global_sums(
+        (current * scaled, scaled * image, image * second, second * second_image)
+    )
+    energy, curve, cross, last = sums[0], sums[1], sums[2], sums[3]
+    step = energy / curve
+    energy_next = step * step * cross - energy
+    ratio = energy_next / energy
+    curve_next = curve - 2.0 * step * cross + step * step * last - ratio * ratio * curve
+    step_next = energy_next / curve_next
+    first_drop = step * scaled
+    direction = (1.0 + ratio) * scaled - step * second
+    along = (1.0 + ratio) * image - step * second_image
+    drop_field = first_drop + step_next * direction
+    resid = current - step * image - step_next * along
+    return (drop_field, resid, jnp.maximum(first_drop, drop_field))
 
 
 def solution(mesh):

time: 249 us -> 160 us (0.64)
  blocking collectives: 148 us -> 54.3 us
  starting transfers between devices: 66.5 us -> 70.2 us
    psum x6 -> x0, blocking collectives: 148 us -> none  [over_axes(): return functools.reduce(lax.psum, axes, value)]
    all_to_all x0 -> x1, blocking collectives: none -> 54.3 us  [global_sums(): return jnp.sum(lax.all_to_all(sent, axes, 0, 0, tiled=True), axis=(0, 1))]
    another operation x0 -> x1, other arithmetic: none -> 2.58 us  [global_sums(): parts = jnp.stack([jnp.sum(field) for field in fields])]
where the time goes in v1:
time: 160 us; the launch traced here: 159 us
  starting transfers between devices  70.2 us (44%)
  blocking collectives  54.3 us (34%)
  other arithmetic  14.6 us (9%)
  waiting for transfers between devices  11.2 us (7%)
  between operations  6.52 us (4%)
  local copies, waits for them, and re-layouts  2.55 us (2%)
    all_to_all x1, blocking collectives, global_sums(): return jnp.sum(lax.all_to_all(sent, axes, 0, 0, tiled=True), axis=(0, 1))  54.3 us
    ppermute x2, starting transfers between devices, from_partner(): lax.ppermute(value, axis, [(i, i ^ 1 << stride) for i in range(lax.axis_s...  42.3 us
    ppermute x6, starting transfers between devices, with_halo(): lax.ppermute(last, axis, up)  20.1 us
    ppermute x6, waiting for transfers between devices, with_halo(): lax.ppermute(initial, axis, [(b, a) for a, b in up])  11.2 us
    ppermute x6, starting transfers between devices, with_halo(): lax.ppermute(initial, axis, [(b, a) for a, b in up])  7.85 us
    add x1, other arithmetic, lookup(): cond + jnp.where(node_class == klass, class_conductance[:, klass][:, None...  6.45 us
  transfers between devices with their start and end apart: 14, of which 3 were waited for; matrix products, arithmetic and copies ran while one was open for 0% of the time, Pallas kernels for 0%

profile of v1, /device:TPU:33, one launch (start us, length us, event | category | flops | bytes accessed | tf_op | source)
XLA Modules:
  0.0 159.4 jit_solution(5655418369072623842)
XLA Ops:
  0.6 1.6 %fusion.46 = (f32[1,1]{1,0:T(1,128)}, f32[1,1]{1,0:T(1,128)}, f32[1,1]{1,0:T(1,128)}, f32[1,1]{1,0:T(1,128)}, f32[1,1]{1,0:T(1,128)}, /*index=5*/f32[1,1]{1,0:T(1,128)}, f32[1,1]{1,0:T(1,128)}, f32[1,1]{1,0:T(1,128)}) fusion(f32[1,8]{1,0:T(1,128)} %param.7), kind=kLoop, calls=%fused_computation.84 | loop fusion | bytes 64 | tf_op jit(solution)/shard_map/slice | solution.py:49
  2.2 0.0 copy-start
  2.2 0.0 copy-start.1
  2.2 6.5 %select_add_fusion = f32[1,128,1024]{2,1,0:T(8,128)S(1)} fusion(s32[1,128,1024]{2,1,0:T(8,128)} %param.6, f32[]{:T(128)} %bitcast.7, f32[]{:T(128)} %bitcast.6, f32[]{:T(128)} %bitcast.5, f32[]{:T(128)} %bitcast.4, f32[]{:T(128)} %bitcast.3, f32[]{:T(128)} %bitcast.2, f32[]{:T(128)} %bitcast.1, f32[]{:T(128)} %bitcast), kind=kLoop, calls=%fused_computation.72 | loop fusion | flops 3014656 | bytes 1048608 | tf_op jit(solution)/shard_map/add | solution.py:48
  8.7 5.2 %collective-permute-start = (f32[1,1,1024]{2,1,0:T(1,128)S(1)}, f32[1,1,1024]{2,1,0:T(1,128)S(1)}, u32[]{:S(2)}, u32[]{:S(2)}) collective-permute-start(f32[1,1,1024]{2,1,0:T(1,128)S(1)} %get-tuple-element.24), channel_id=1, source_target_pairs={{0,8},{8,16},{16,24},{24,32},{32,40},{40,48},{48,56},{56,64},{64,7... | collective-permute-start | bytes 12296 | tf_op jit(solution)/shard_map/ppermute | solution.py:19
  14.0 1.3 collective-permute-start.1
  15.3 0.1 fusion.43
  15.4 3.3 %collective-permute-start.2 = (f32[1,128,1]{2,1,0:T(8,128)S(1)}, f32[1,128,1]{2,1,0:T(8,128)S(1)}, u32[]{:S(2)}, u32[]{:S(2)}) collective-permute-start(f32[1,128,1]{2,1,0:T(8,128)S(1)} %get-tuple-element.22), channel_id=1, source_target_pairs={{0,2},{2,4},{4,6},{1,3},{3,5},{5,7},{8,10},{10,12},{12,14},{9,11},... | collective-permute-start | bytes 1544 | tf_op jit(solution)/shard_map/ppermute | solution.py:19
  18.6 1.3 collective-permute-start.3
  20.0 0.0 collective-permute-done.2
  20.0 3.7 %collective-permute-done.3 = f32[1,128,1]{2,1,0:T(8,128)S(1)} collective-permute-done((f32[1,128,1]{2,1,0:T(8,128)S(1)}, f32[1,128,1]{2,1,0:T(8,128)S(1)}, u32[]{:S(2)}, u32[]{:S(2)}) %collective-permute-start.3) | collective-permute-done | bytes 544 | tf_op jit(solution)/shard_map/ppermute | solution.py:20
  23.7 0.0 collective-permute-done
  23.7 0.0 collective-permute-done.1
  23.7 0.0 copy-done
  23.7 0.0 copy-done.1
  23.7 1.7 %fusion.37 = (f32[1,128,1024]{2,1,0:T(8,128)S(1)}, f32[1,128,1024]{2,1,0:T(8,128)S(1)}) fusion(f32[1,128,1024]{2,1,0:T(8,128)S(1)} %copy-done.1, s32[1,128,1024]{2,1,0:T(8,128)} %param.8, s32[128,1024]{1,0:T(8,128)S(1)} %copy-done, f32[1,128,1024]{2,1,0:T(8,128)S(1)} %select_add_fusion, f32[1,128,1]{2,1,0:T(8,128)S(1)} %collective-permute-done.3, ...), kind=kLoop, calls=%fused_computation.76 | loop fusion | flops 5373952 | bytes 3154944 | tf_op jit(solution)/shard_map/div | solution.py:88
  25.4 38.6 %collective-permute-start.8 = (f32[1,128,1024]{2,1,0:T(8,128)S(1)}, f32[1,128,1024]{2,1,0:T(8,128)S(1)}, u32[]{:S(2)}, u32[]{:S(2)}) collective-permute-start(f32[1,128,1024]{2,1,0:T(8,128)S(1)} %get-tuple-element.12), channel_id=1, source_target_pairs={{0,1},{1,0},{2,3},{3,2},{4,5},{5,4},{6,7},{7,6},{8,9},{9,8},{10,11... | collective-permute-start | bytes 1572872 | tf_op jit(solution)/shard_map/ppermute | solution.py:32
  64.0 4.3 %collective-permute-start.4 = (f32[1,1,1024]{2,1,0:T(1,128)S(1)}, f32[1,1,1024]{2,1,0:T(1,128)S(1)}, u32[]{:S(2)}, u32[]{:S(2)}) collective-permute-start(f32[1,1,1024]{2,1,0:T(1,128)S(1)} %get-tuple-element.20), channel_id=1, source_target_pairs={{0,8},{8,16},{16,24},{24,32},{32,40},{40,48},{48,56},{56,64},{64,7... | collective-permute-start | bytes 12296 | tf_op jit(solution)/shard_map/ppermute | solution.py:19
  68.3 1.3 collective-permute-start.5
  69.6 0.1 fusion.41
  69.7 1.3 collective-permute-start.6
  71.0 1.3 collective-permute-start.7
  72.4 0.0 collective-permute-done.6
  72.4 3.7 %collective-permute-done.7 = f32[1,128,1]{2,1,0:T(8,128)S(1)} collective-permute-done((f32[1,128,1]{2,1,0:T(8,128)S(1)}, f32[1,128,1]{2,1,0:T(8,128)S(1)}, u32[]{:S(2)}, u32[]{:S(2)}) %collective-permute-start.7) | collective-permute-done | bytes 544 | tf_op jit(solution)/shard_map/ppermute | solution.py:20
  76.1 0.0 collective-permute-done.4
  76.1 0.0 collective-permute-done.5
  76.1 0.0 collective-permute-done.8
  76.1 0.8 fusion.35
  76.9 3.7 %collective-permute-start.13 = (f32[1,128,1024]{2,1,0:T(8,128)S(1)}, f32[1,128,1024]{2,1,0:T(8,128)S(1)}, u32[]{:S(2)}, u32[]{:S(2)}) collective-permute-start(f32[1,128,1024]{2,1,0:T(8,128)S(1)} %get-tuple-element.10), channel_id=1, source_target_pairs={{0,1},{1,0},{2,3},{3,2},{4,5},{5,4},{6,7},{7,6},{8,9},{9,8},{10,11... | collective-permute-start | bytes 1572872 | tf_op jit(solution)/shard_map/ppermute | solution.py:32
  80.6 4.3 %collective-permute-start.9 = (f32[1,1,1024]{2,1,0:T(1,128)S(1)}, f32[1,1,1024]{2,1,0:T(1,128)S(1)}, u32[]{:S(2)}, u32[]{:S(2)}) collective-permute-start(f32[1,1,1024]{2,1,0:T(1,128)S(1)} %get-tuple-element.16), channel_id=1, source_target_pairs={{0,8},{8,16},{16,24},{24,32},{32,40},{40,48},{48,56},{56,64},{64,7... | collective-permute-start | bytes 12296 | tf_op jit(solution)/shard_map/ppermute | solution.py:19
  84.9 1.3 collective-permute-start.10
  86.3 0.1 fusion.39
  86.3 1.7 %collective-permute-start.11 = (f32[1,128,1]{2,1,0:T(8,128)S(1)}, f32[1,128,1]{2,1,0:T(8,128)S(1)}, u32[]{:S(2)}, u32[]{:S(2)}) collective-permute-start(f32[1,128,1]{2,1,0:T(8,128)S(1)} %get-tuple-element.14), channel_id=1, source_target_pairs={{0,2},{2,4},{4,6},{1,3},{3,5},{5,7},{8,10},{10,12},{12,14},{9,11},... | collective-permute-start | bytes 1544 | tf_op jit(solution)/shard_map/ppermute | solution.py:19
  88.0 1.3 collective-permute-start.12
  89.3 0.0 collective-permute-done.11
  89.3 3.7 %collective-permute-done.12 = f32[1,128,1]{2,1,0:T(8,128)S(1)} collective-permute-done((f32[1,128,1]{2,1,0:T(8,128)S(1)}, f32[1,128,1]{2,1,0:T(8,128)S(1)}, u32[]{:S(2)}, u32[]{:S(2)}) %collective-permute-start.12) | collective-permute-done | bytes 544 | tf_op jit(solution)/shard_map/ppermute | solution.py:20
  93.1 0.0 collective-permute-done.9
  93.1 0.0 collective-permute-done.10
  93.1 0.0 collective-permute-done.13
  93.1 1.5 multiply_reduce_fusion.3
  94.6 2.6 %pad_maximum_fusion.18 = f32[4]{0:T(128)S(1)} fusion(f32[1]{0:T(128)} %bitcast.12, f32[1]{0:T(128)} %bitcast.11, f32[1]{0:T(128)} %bitcast.10, f32[1]{0:T(128)} %bitcast.9), kind=kLoop, calls=%fused_computation.74 | loop fusion | flops 12 | bytes 32 | tf_op jit(solution)/shard_map/stack | solution.py:40
  97.2 0.1 broadcast_in_dim.104
  97.3 54.3 %all_to_all.5 = f32[256,1,4]{2,1,0:T(1,128)S(1)} all-to-all(f32[256,1,4]{2,1,0:T(1,128)S(1)} %broadcast_in_dim.104), channel_id=1, replica_groups=mesh['scen'=2,'row'=32,'col'=4,'layer'=2] {'row','col','layer'}, dimensions={0} | all-to-all | bytes 8192 | tf_op jit(solution)/shard_map/all_to_all | solution.py:42
  151.5 0.3 reduce_sum.49
  151.8 0.6 fusion.45
  158.1 1.3 multiply_maximum_fusion
  (3 shorter events, 0.0 us)
Async XLA Ops:
  2.2 21.5 %copy-start = (s32[128,1024]{1,0:T(8,128)S(1)}, s32[128,1024]{1,0:T(8,128)}, u32[]{:S(2)}) copy-start(s32[128,1024]{1,0:T(8,128)} %param.9) | copy-start | bytes 1572868
  2.2 21.5 %copy-start.1 = (f32[1,128,1024]{2,1,0:T(8,128)S(1)}, f32[1,128,1024]{2,1,0:T(8,128)}, u32[]{:S(2)}) copy-start(f32[1,128,1024]{2,1,0:T(8,128)} %param.5) | copy-start | bytes 1572868
  8.7 15.0 %collective-permute-start = (f32[1,1,1024]{2,1,0:T(1,128)S(1)}, f32[1,1,1024]{2,1,0:T(1,128)S(1)}, u32[]{:S(2)}, u32[]{:S(2)}) collective-permute-start(f32[1,1,1024]{2,1,0:T(1,128)S(1)} %get-tuple-element.24), channel_id=1, source_target_pairs={{0,8},{8,16},{16,24},{24,32},{32,40},{40,48},{48,56},{56,64},{64,7... | collective-permute-start | bytes 12296 | tf_op jit(solution)/shard_map/ppermute | solution.py:19
  14.0 9.7 %collective-permute-start.1 = (f32[1,1,1024]{2,1,0:T(1,128)S(1)}, f32[1,1,1024]{2,1,0:T(1,128)S(1)}, u32[]{:S(2)}, u32[]{:S(2)}) collective-permute-start(f32[1,1,1024]{2,1,0:T(1,128)S(1)} %get-tuple-element.25), channel_id=1, source_target_pairs={{8,0},{16,8},{24,16},{32,24},{40,32},{48,40},{56,48},{64,56},{72,6... | collective-permute-start | bytes 12296 | tf_op jit(solution)/shard_map/ppermute | solution.py:20
  15.4 4.6 %collective-permute-start.2 = (f32[1,128,1]{2,1,0:T(8,128)S(1)}, f32[1,128,1]{2,1,0:T(8,128)S(1)}, u32[]{:S(2)}, u32[]{:S(2)}) collective-permute-start(f32[1,128,1]{2,1,0:T(8,128)S(1)} %get-tuple-element.22), channel_id=1, source_target_pairs={{0,2},{2,4},{4,6},{1,3},{3,5},{5,7},{8,10},{10,12},{12,14},{9,11},... | collective-permute-start | bytes 1544 | tf_op jit(solution)/shard_map/ppermute | solution.py:19
  18.6 5.0 %collective-permute-start.3 = (f32[1,128,1]{2,1,0:T(8,128)S(1)}, f32[1,128,1]{2,1,0:T(8,128)S(1)}, u32[]{:S(2)}, u32[]{:S(2)}) collective-permute-start(f32[1,128,1]{2,1,0:T(8,128)S(1)} %get-tuple-element.23), channel_id=1, source_target_pairs={{2,0},{4,2},{6,4},{3,1},{5,3},{7,5},{10,8},{12,10},{14,12},{11,9},... | collective-permute-start | bytes 1544 | tf_op jit(solution)/shard_map/ppermute | solution.py:20
  25.4 50.7 %collective-permute-start.8 = (f32[1,128,1024]{2,1,0:T(8,128)S(1)}, f32[1,128,1024]{2,1,0:T(8,128)S(1)}, u32[]{:S(2)}, u32[]{:S(2)}) collective-permute-start(f32[1,128,1024]{2,1,0:T(8,128)S(1)} %get-tuple-element.12), channel_id=1, source_target_pairs={{0,1},{1,0},{2,3},{3,2},{4,5},{5,4},{6,7},{7,6},{8,9},{9,8},{10,11... | collective-permute-start | bytes 1572872 | tf_op jit(solution)/shard_map/ppermute | solution.py:32
  64.0 12.1 %collective-permute-start.4 = (f32[1,1,1024]{2,1,0:T(1,128)S(1)}, f32[1,1,1024]{2,1,0:T(1,128)S(1)}, u32[]{:S(2)}, u32[]{:S(2)}) collective-permute-start(f32[1,1,1024]{2,1,0:T(1,128)S(1)} %get-tuple-element.20), channel_id=1, source_target_pairs={{0,8},{8,16},{16,24},{24,32},{32,40},{40,48},{48,56},{56,64},{64,7... | collective-permute-start | bytes 12296 | tf_op jit(solution)/shard_map/ppermute | solution.py:19
  68.3 7.8 %collective-permute-start.5 = (f32[1,1,1024]{2,1,0:T(1,128)S(1)}, f32[1,1,1024]{2,1,0:T(1,128)S(1)}, u32[]{:S(2)}, u32[]{:S(2)}) collective-permute-start(f32[1,1,1024]{2,1,0:T(1,128)S(1)} %get-tuple-element.21), channel_id=1, source_target_pairs={{8,0},{16,8},{24,16},{32,24},{40,32},{48,40},{56,48},{64,56},{72,6... | collective-permute-start | bytes 12296 | tf_op jit(solution)/shard_map/ppermute | solution.py:20
  69.7 2.6 %collective-permute-start.6 = (f32[1,128,1]{2,1,0:T(8,128)S(1)}, f32[1,128,1]{2,1,0:T(8,128)S(1)}, u32[]{:S(2)}, u32[]{:S(2)}) collective-permute-start(f32[1,128,1]{2,1,0:T(8,128)S(1)} %get-tuple-element.18), channel_id=1, source_target_pairs={{0,2},{2,4},{4,6},{1,3},{3,5},{5,7},{8,10},{10,12},{12,14},{9,11},... | collective-permute-start | bytes 1544 | tf_op jit(solution)/shard_map/ppermute | solution.py:19
  71.0 5.0 %collective-permute-start.7 = (f32[1,128,1]{2,1,0:T(8,128)S(1)}, f32[1,128,1]{2,1,0:T(8,128)S(1)}, u32[]{:S(2)}, u32[]{:S(2)}) collective-permute-start(f32[1,128,1]{2,1,0:T(8,128)S(1)} %get-tuple-element.19), channel_id=1, source_target_pairs={{2,0},{4,2},{6,4},{3,1},{5,3},{7,5},{10,8},{12,10},{14,12},{11,9},... | collective-permute-start | bytes 1544 | tf_op jit(solution)/shard_map/ppermute | solution.py:20
  76.9 16.1 %collective-permute-start.13 = (f32[1,128,1024]{2,1,0:T(8,128)S(1)}, f32[1,128,1024]{2,1,0:T(8,128)S(1)}, u32[]{:S(2)}, u32[]{:S(2)}) collective-permute-start(f32[1,128,1024]{2,1,0:T(8,128)S(1)} %get-tuple-element.10), channel_id=1, source_target_pairs={{0,1},{1,0},{2,3},{3,2},{4,5},{5,4},{6,7},{7,6},{8,9},{9,8},{10,11... | collective-permute-start | bytes 1572872 | tf_op jit(solution)/shard_map/ppermute | solution.py:32
  80.6 12.4 %collective-permute-start.9 = (f32[1,1,1024]{2,1,0:T(1,128)S(1)}, f32[1,1,1024]{2,1,0:T(1,128)S(1)}, u32[]{:S(2)}, u32[]{:S(2)}) collective-permute-start(f32[1,1,1024]{2,1,0:T(1,128)S(1)} %get-tuple-element.16), channel_id=1, source_target_pairs={{0,8},{8,16},{16,24},{24,32},{32,40},{40,48},{48,56},{56,64},{64,7... | collective-permute-start | bytes 12296 | tf_op jit(solution)/shard_map/ppermute | solution.py:19
  84.9 8.1 %collective-permute-start.10 = (f32[1,1,1024]{2,1,0:T(1,128)S(1)}, f32[1,1,1024]{2,1,0:T(1,128)S(1)}, u32[]{:S(2)}, u32[]{:S(2)}) collective-permute-start(f32[1,1,1024]{2,1,0:T(1,128)S(1)} %get-tuple-element.17), channel_id=1, source_target_pairs={{8,0},{16,8},{24,16},{32,24},{40,32},{48,40},{56,48},{64,56},{72,6... | collective-permute-start | bytes 12296 | tf_op jit(solution)/shard_map/ppermute | solution.py:20
  86.3 3.0 %collective-permute-start.11 = (f32[1,128,1]{2,1,0:T(8,128)S(1)}, f32[1,128,1]{2,1,0:T(8,128)S(1)}, u32[]{:S(2)}, u32[]{:S(2)}) collective-permute-start(f32[1,128,1]{2,1,0:T(8,128)S(1)} %get-tuple-element.14), channel_id=1, source_target_pairs={{0,2},{2,4},{4,6},{1,3},{3,5},{5,7},{8,10},{10,12},{12,14},{9,11},... | collective-permute-start | bytes 1544 | tf_op jit(solution)/shard_map/ppermute | solution.py:19
  88.0 5.0 %collective-permute-start.12 = (f32[1,128,1]{2,1,0:T(8,128)S(1)}, f32[1,128,1]{2,1,0:T(8,128)S(1)}, u32[]{:S(2)}, u32[]{:S(2)}) collective-permute-start(f32[1,128,1]{2,1,0:T(8,128)S(1)} %get-tuple-element.15), channel_id=1, source_target_pairs={{2,0},{4,2},{6,4},{3,1},{5,3},{7,5},{10,8},{12,10},{14,12},{11,9},... | collective-permute-start | bytes 1544 | tf_op jit(solution)/shard_map/ppermute | solution.py:20

commit v2 on v1

v2 whole, which is shorter than its diff:
```python
import functools

import jax
import jax.numpy as jnp
from jax import lax
from jax.experimental import pallas as pl
from jax.experimental.pallas import tpu as pltpu
from jax.sharding import PartitionSpec as P

via_conductance = 2.0
pad_conductance = 4.0
leakage = 0.05

SUB = 8
LANE = 128


def lanes_of(shape):
    return lax.broadcasted_iota(jnp.int32, shape, len(shape) - 1)


def rows_of(shape):
    return lax.broadcasted_iota(jnp.int32, shape, len(shape) - 2)


def turned(value, shift, axis):
    size = value.shape[axis]
    return pltpu.roll(value, shift % size, axis) if shift % size else value


def conductance(classes, table):
    cond = jnp.zeros(classes.shape, jnp.float32)
    for klass in range(table.shape[1]):
        cond = jnp.where(classes == klass, table[0, klass], cond)
    return cond


def pad_term(pads):
    return pad_conductance * pads.astype(jnp.float32) + leakage


def via_term(vias):
    return via_conductance * vias.astype(jnp.float32)


def border_rows(table, top, bottom):
    out = []
    for blocks, shifts, far in ((top, (0, 3, 5, 7), 1), (bottom, (3, 5, 7, 0), SUB - 2)):
        classes, current, pads, vias = blocks
        row = rows_of(current.shape)
        cond = conductance(classes, table)
        coupling = via_term(vias)
        own = pad_term(pads)
        own = jnp.where(row == far, own + coupling, own)
        parts = [turned(v, s, 0) for v, s in zip((cond, current, own, coupling), shifts)]
        out.append(
            jnp.where(row < 3, parts[0], jnp.where(row < 5, parts[1], jnp.where(row < 7, parts[2], parts[3])))
        )
    return out


def rows_kernel(table, ct, rt, pt, vt, cb, rb, pb, vb, up, down):
    up[...], down[...] = border_rows(
        table, (ct[0], rt[0], pt[0], vt[...]), (cb[0], rb[0], pb[0], vb[...])
    )


def border_columns(low, high):
    lane = lanes_of(low[0].shape)
    out = None
    for blocks, shifts, far, start in ((high, (3, 5, 7, 8), LANE - 2, 0), (low, (8, 11, 13, 15), 1, 8)):
        cond, current, own, coupling = blocks
        own = jnp.where(lane == far, own + coupling, own)
        parts = [turned(v, s, 1) for v, s in zip((cond, current, own, coupling), shifts)]
        at = lane - start
        side = jnp.where(at < 3, parts[0], jnp.where(at < 5, parts[1], jnp.where(at < 7, parts[2], parts[3])))
        out = side if out is None else jnp.where(lane < start, out, side)
    return out


def tile_kernel(table, classes, current, pads, vias, bulk, strips):
    rows, width = vias.shape

    def strip(s, carry):
        at = pl.ds(pl.multiple_of(s * SUB, SUB), SUB)
        bulk[0, at, :] = conductance(classes[0, at, :], table)
        bulk[1, at, :] = current[0, at, :]
        bulk[2, at, :] = pad_term(pads[0, at, :])
        return carry

    lax.fori_loop(0, rows // SUB, strip, 0)
    sides = [
        (bulk[0, :, at], bulk[1, :, at], bulk[2, :, at], via_term(vias[:, at]))
        for at in (slice(0, LANE), slice(width - LANE, width))
    ]
    strips[...] = border_columns(*sides).T[: 2 * SUB]


def spread_rows(message, below):
    shifts, firsts = ((0, 5, 3, 1), (0, 0, 0, 0)) if below else ((5, 3, 1, 0), (5, 6, 6, 7))
    counts = (3, 2, 2, 1)
    row = rows_of(message.shape)
    return [
        jnp.where((row >= f) & (row < f + n), turned(message, s, 0), 0.0)
        for s, f, n in zip(shifts, firsts, counts)
    ]


def send_kernel(place, top, bottom, strips, send):
    width = top.shape[1]
    blocks = []
    for at in (slice(0, LANE), slice(width - LANE, width)):
        above = spread_rows(top[:, at], False)
        under = spread_rows(bottom[:, at], True)
        blocks.append([jnp.concatenate([a, b], axis=0) for a, b in zip(above, under)])
    around = border_columns(*blocks)
    around = jnp.concatenate([around, jnp.zeros((LANE - 2 * SUB, LANE), jnp.float32)], axis=0).T
    high = jnp.concatenate([strips[:SUB], around[:SUB]], axis=1)
    low = jnp.concatenate([strips[SUB:], around[SUB : 2 * SUB]], axis=1)
    for k in range(send.shape[0]):
        send[k] = jnp.where(k // 2 > place[0], high, low)


def side_lanes(left, right):
    fill = jnp.zeros((LANE - 2 * SUB, LANE), jnp.float32)
    both = jnp.concatenate([left, right, fill], axis=0).T
    lane = lanes_of(both.shape)
    out = []
    for first, before, after in ((0, 3, 3), (3, 2, 2), (5, 2, 2), (7, 1, 1)):
        low = turned(both, LANE - before - first, 1)
        high = turned(both, -SUB - first, 1)
        out.append(jnp.where(lane >= LANE - before, low, jnp.where(lane < after, high, 0.0)))
    return out


def grid_kernel(
    place, own, other, vias, top, bottom, frames, recv,
    z_out, u_out, w_out, v_out, sums,
    cond, resid, extra, coup, eh, ev, inv, z, u, flux,
):
    rows, width = vias.shape
    strips = rows // SUB
    wide = width + LANE
    columns = recv.shape[0] // 2

    def at(s):
        return pl.ds(pl.multiple_of((s + 1) * SUB, SUB), SUB)

    for layer in range(2):
        source = own if layer == 0 else other
        mine = place[1] if layer == 0 else 1 - place[1]
        c = place[0]
        left = recv[jnp.maximum(2 * (c - 1) + mine, 0)]
        left = jnp.where(c > 0, left, 0.0)
        right = recv[jnp.minimum(2 * (c + 1) + mine, 2 * columns - 1)]
        right = jnp.where(c < columns - 1, right, 0.0)
        beside = side_lanes(left[:, :LANE], right[:, :LANE])
        corner = side_lanes(left[:, LANE:], right[:, LANE:])
        above = spread_rows(top[...] if layer == 0 else frames[:SUB], False)
        under = spread_rows(bottom[...] if layer == 0 else frames[SUB:], True)
        fields = [cond, resid, extra] + ([coup] if layer == 0 else [])
        for k, field in enumerate(fields):
            to = field.at[layer] if k < 3 else field
            to[SUB : 2 * SUB, :width] = above[k]
            to[(strips + 2) * SUB : (strips + 3) * SUB, :width] = under[k]
            to[SUB : 2 * SUB, width:] = corner[k][:SUB]
            to[(strips + 2) * SUB : (strips + 3) * SUB, width:] = corner[k][SUB : 2 * SUB]
            to[2 * SUB : (strips + 2) * SUB, width:] = beside[k]
            if k < 3:
                to[2 * SUB : (strips + 2) * SUB, :width] = source[k]
            else:
                to[2 * SUB : (strips + 2) * SUB, :width] = via_term(vias[...])

    row = rows_of((SUB, wide))
    first, last = row == 0, row == SUB - 1

    def after(value):
        return turned(value, -1, 1)

    def before(value):
        return turned(value, 1, 1)

    def below(value, following):
        return turned(jnp.where(first, following, value), -1, 0)

    def above_of(value, preceding):
        return turned(jnp.where(last, preceding, value), 1, 0)

    def edge(a, b):
        return jnp.where((a > 0.0) & (b > 0.0), 0.5 * (a + b), 0.0)

    def scale(s, carry):
        k = coup[at(s), :]
        for layer in range(2):
            c = cond[layer, at(s), :]
            h = edge(c, after(c))
            v = edge(c, below(c, cond[layer, at(s + 1), :]))
            eh[layer, at(s), :] = h
            ev[layer, at(s), :] = v
            diagonal = h + before(h) + v + above_of(v, ev[layer, at(s - 1), :]) + k + extra[layer, at(s), :]
            inverse = jnp.where(c > 0.0, 1.0 / diagonal, 0.0)
            inv[layer, at(s), :] = inverse
            z[layer, at(s), :] = resid[layer, at(s), :] * inverse
        return carry

    lax.fori_loop(0, strips + 2, scale, 0)

    def folded(value):
        parts = [value[:, i * LANE : (i + 1) * LANE] for i in range(width // LANE)]
        while len(parts) > 1:
            parts = [a + b for a, b in zip(parts[::2], parts[1::2])]
        return parts[0]

    def image(field, s, layer, k):
        x = field[layer, at(s), :]
        fh = eh[layer, at(s), :] * (x - after(x))
        fv = ev[layer, at(s), :] * (x - below(x, field[layer, at(s + 1), :]))
        previous = flux[layer, at(s - 1), :]
        flux[layer, at(s), :] = fv
        there = field[1 - layer, at(s), :]
        return x, fh - before(fh) + fv - above_of(fv, previous) + k * (x - there) + extra[layer, at(s), :] * x

    def second(s, keep):
        k = coup[at(s), :]
        found = []
        for layer in range(2):
            x, w = image(z, s, layer, k)
            y = w * inv[layer, at(s), :]
            u[layer, at(s), :] = y
            found.append((x, w, y))
        if not keep:
            return None
        to = pl.ds(pl.multiple_of((s - 1) * SUB, SUB), SUB)
        z_out[to, :] = found[0][0][:, :width]
        w_out[to, :] = found[0][1][:, :width]
        u_out[to, :] = found[0][2][:, :width]
        energy = folded(sum(resid[i, at(s), :] * found[i][0] for i in range(2)))
        curve = folded(sum(found[i][0] * found[i][1] for i in range(2)))
        cross = folded(sum(found[i][1] * found[i][2] for i in range(2)))
        return energy, curve, cross

    zero = jnp.zeros((SUB, LANE), jnp.float32)
    second(0, False)
    totals = lax.fori_loop(
        1, strips + 1, lambda s, t: tuple(a + b for a, b in zip(t, second(s, True))), (zero,) * 3
    )
    second(strips + 1, False)

    x = u[0, at(0), :]
    flux[0, at(0), :] = ev[0, at(0), :] * (x - below(x, u[0, at(1), :]))

    def third(s, total):
        k = coup[at(s), :]
        x, v = image(u, s, 0, k)
        to = pl.ds(pl.multiple_of((s - 1) * SUB, SUB), SUB)
        v_out[to, :] = v[:, :width]
        y = u[1, at(s), :]
        dh = y - after(y)
        dv = y - below(y, u[1, at(s + 1), :])
        there = eh[1, at(s), :] * dh * dh + ev[1, at(s), :] * dv * dv
        there = there + y * (k * (y - x) + extra[1, at(s), :] * y)
        return total + folded(x * v + there)

    total = lax.fori_loop(1, strips + 1, third, zero)
    lane = lanes_of((1, LANE))
    line = jnp.zeros((1, LANE), jnp.float32)
    for k, value in enumerate(totals + (total,)):
        line = jnp.where(lane == k, jnp.sum(value, axis=(0, 1), keepdims=True), line)
    sums[...] = jnp.broadcast_to(line[None], sums.shape)


def finish_kernel(parts, current, z, u, w, v, drop, resid, worst):
    line = jnp.sum(parts[...], axis=0)
    lane = lanes_of(line.shape)
    energy, curve, cross, last = (
        jnp.sum(jnp.where(lane == k, line, 0.0), axis=1, keepdims=True) for k in range(4)
    )
    step = energy / curve
    energy_next = step * step * cross - energy
    ratio = energy_next / energy
    curve_next = curve - 2.0 * step * cross + step * step * last - ratio * ratio * curve
    step_next = energy_next / curve_next
    keep = 1.0 + ratio
    first_drop = step * z[...]
    second_drop = first_drop + step_next * (keep * z[...] - step * u[...])
    drop[0] = second_drop
    worst[0] = jnp.maximum(first_drop, second_drop)
    resid[0] = current[0] - step * w[...] - step_next * (keep * w[...] - step * v[...])


def local(current, node_class, class_conductance, pad_mask, via_mask):
    _, rows, width = current.shape
    n_row, n_col = lax.axis_size("row"), lax.axis_size("col")
    up_pairs = [(i, i + 1) for i in range(n_row - 1)]
    down_pairs = [(b, a) for a, b in up_pairs]
    swap = [(0, 1), (1, 0)]
    place = jnp.stack([lax.axis_index("col"), lax.axis_index("layer")]).astype(jnp.int32)
    f32 = jnp.float32
    smem = pl.BlockSpec(memory_space=pltpu.SMEM)
    vmem = pl.BlockSpec(memory_space=pltpu.VMEM)

    def shape(*dims):
        return jax.ShapeDtypeStruct(dims, f32)

    def ends(index):
        block = pl.BlockSpec((1, SUB, width), lambda i: (0, index, 0))
        return [block] * 3 + [pl.BlockSpec((SUB, width), lambda i: (index, 0))]

    fields = (node_class, current, pad_mask, via_mask)
    message = pl.BlockSpec((SUB, width), lambda i: (0, 0))
    up, down = pl.pallas_call(
        rows_kernel,
        grid=(1,),
        in_specs=[smem] + ends(0) + ends(rows // SUB - 1),
        out_specs=[message] * 2,
        out_shape=[shape(SUB, width)] * 2,
        name="border_rows",
    )(class_conductance, *fields, *fields)
    top = lax.ppermute(down, "row", up_pairs)
    bottom = lax.ppermute(up, "row", down_pairs)

    bulk, strips = pl.pallas_call(
        tile_kernel,
        in_specs=[smem] + [vmem] * 4,
        out_specs=[vmem] * 2,
        out_shape=[shape(3, rows, width), shape(2 * SUB, LANE)],
        name="tile_fields",
    )(class_conductance, *fields)
    other = lax.ppermute(bulk, "layer", swap)

    frames = lax.ppermute(jnp.concatenate([top, bottom], axis=0), "layer", swap)
    send = pl.pallas_call(
        send_kernel,
        in_specs=[smem] + [vmem] * 3,
        out_specs=vmem,
        out_shape=shape(2 * n_col, SUB, 2 * LANE),
        name="border_columns",
    )(place, top, bottom, strips)
    recv = lax.all_to_all(send, ("col", "layer"), 0, 0, tiled=True)

    full = (rows + 4 * SUB, width + LANE)
    pair = pltpu.VMEM((2,) + full, f32)
    z, u, w, v, sums = pl.pallas_call(
        grid_kernel,
        in_specs=[smem] + [vmem] * 7,
        out_specs=[vmem] * 5,
        out_shape=[shape(rows, width)] * 4 + [shape(n_row * n_col, 1, LANE)],
        scratch_shapes=[pair, pair, pair, pltpu.VMEM(full, f32)] + [pair] * 6,
        name="grid",
    )(place, bulk, other, via_mask, top, bottom, frames, recv)
    parts = lax.all_to_all(sums, ("row", "col"), 0, 0, tiled=True)

    pieces = 4
    part = rows // pieces
    flat = pl.BlockSpec((part, width), lambda i: (i, 0))
    deep = pl.BlockSpec((1, part, width), lambda i: (0, i, 0))
    return pl.pallas_call(
        finish_kernel,
        grid=(pieces,),
        in_specs=[pl.BlockSpec(parts.shape, lambda i: (0, 0, 0)), deep] + [flat] * 4,
        out_specs=[deep] * 3,
        out_shape=[shape(1, rows, width)] * 3,
        name="finish",
    )(parts, current, z, u, w, v)


def solution(mesh):
    tile = P("layer", ("scen", "row"), "col")
    in_specs = (tile, tile, P("layer", None), tile, P(("scen", "row"), "col"))
    return jax.shard_map(local, mesh=mesh, in_specs=in_specs, out_specs=(tile,) * 3, check_vma=False)
```

time: 160 us -> 126 us (0.79); the launches traced: 159 us -> 124 us
  Pallas kernels: 0 us -> 23.7 us
  starting transfers between devices: 70.2 us -> 49.1 us
  other arithmetic: 14.6 us -> 0.66 us
  blocking collectives: 54.3 us -> 44.2 us
  waiting for transfers between devices: 11.2 us -> 3.56 us
  between operations: 6.52 us -> 0.7 us
    pallas_call x0 -> x5, Pallas kernels: none -> 23.7 us  [the longest x1 13.1 us: local(): pl.pallas_call(grid_kernel, in_specs=[smem] + [vmem] * 7, out_specs=[vmem...]
    ppermute x14 -> x4, starting transfers between devices: 70.2 us -> 49.1 us  [the longest x1 43.4 us: local(): other = lax.ppermute(bulk, 'layer', swap)]
    all_to_all x1 -> x2, blocking collectives: 54.3 us -> 44.2 us  [the longest x1 35.3 us: local(): parts = lax.all_to_all(sums, ('row', 'col'), 0, 0, tiled=True)]
    ppermute x14 -> x4, waiting for transfers between devices: 11.2 us -> 3.56 us  [the longest x1 3.56 us: local(): bottom = lax.ppermute(up, 'row', down_pairs)]
    add x1 -> x0, other arithmetic: 6.45 us -> none  [lookup(): cond + jnp.where(node_class == klass, class_conductance[:, klass][:, None...]
    div x2 -> x0, other arithmetic: 2.51 us -> none  [the longest x1 1.67 us: local(): scaled = current / diagonal]
    slice x8 -> x0, local copies, waits for them, and re-layouts: 2.47 us -> none  [the longest x1 1.6 us: lookup(): class_conductance[:, klass][:, None, None]]
    another operation x1, other arithmetic: 2.58 us -> 0.65 us  [local(): jnp.stack([lax.axis_index('col'), lax.axis_index('layer')])]
  transfers between devices with their start and end apart: 14 -> 4, of which waited for: 3 -> 1; matrix products, arithmetic and copies ran while one was open for 0% -> 1% of each run, Pallas kernels for 0% -> 3%
where the time goes in v2:
time: 126 us; the launch traced here: 124 us
  starting transfers between devices  49.1 us (39%)
  blocking collectives  44.2 us (35%)
  Pallas kernels  23.7 us (19%)
  waiting for transfers between devices  3.56 us (3%)
  local copies, waits for them, and re-layouts  1.79 us (1%)
    ppermute x1, starting transfers between devices, local(): other = lax.ppermute(bulk, 'layer', swap)  43.4 us
    all_to_all x1, blocking collectives, local(): parts = lax.all_to_all(sums, ('row', 'col'), 0, 0, tiled=True)  35.3 us
    pallas_call x1, Pallas kernels, local(): pl.pallas_call(grid_kernel, in_specs=[smem] + [vmem] * 7, out_specs=[vmem...  13.1 us
    all_to_all x1, blocking collectives, local(): recv = lax.all_to_all(send, ('col', 'layer'), 0, 0, tiled=True)  8.87 us
    pallas_call x1, Pallas kernels, local(): pl.pallas_call(finish_kernel, grid=(pieces,), in_specs=[pl.BlockSpec(part...  4.37 us
    ppermute x1, waiting for transfers between devices, local(): bottom = lax.ppermute(up, 'row', down_pairs)  3.56 us
    pallas_call x1, Pallas kernels, local(): pl.pallas_call(tile_kernel, in_specs=[smem] + [vmem] * 4, out_specs=[vmem...  3.11 us
    ppermute x1, starting transfers between devices, local(): frames = lax.ppermute(jnp.concatenate([top, bottom], axis=0), 'layer', swap)  3.1 us
  transfers between devices with their start and end apart: 4, of which 1 were waited for; matrix products, arithmetic and copies ran while one was open for 1% of the time, Pallas kernels for 3%

profile of v2, /device:TPU:33, one launch (start us, length us, event | category | flops | bytes accessed | tf_op | source)
XLA Modules:
  0.0 123.7 jit_solution(12398472424702013845)
XLA Ops:
  0.6 3.1 %tile_fields.1 = (f32[3,128,1024]{2,1,0:T(8,128)}, f32[16,128]{1,0:T(8,128)}) custom-call(f32[1,8]{1,0:T(1,128)} %table.3, s32[1,128,1024]{2,1,0:T(8,128)} %cb.1, f32[1,128,1024]{2,1,0:T(8,128)} %current.3, s32[1,128,1024]{2,1,0:T(8,128)} %pb.1, s32[128,1024]{1,0:T(8,128)} %vias.3), custom_call_target="tpu_custom_call" | custom-call | tf_op jit(solution)/shard_map/tile_fields/pallas_call | solution.py:322
  3.7 43.4 %collective-permute-start = (f32[3,128,1024]{2,1,0:T(8,128)}, f32[3,128,1024]{2,1,0:T(8,128)S(1)}, u32[]{:S(2)}, u32[]{:S(2)}) collective-permute-start(f32[3,128,1024]{2,1,0:T(8,128)} %get-tuple-element.12.own), channel_id=1, source_target_pairs={{0,1},{1,0},{2,3},{3,2},{4,5},{5,4},{6,7},{7,6},{8,9},{9,8},{10,11... | collective-permute-start | bytes 4718600 | tf_op jit(solution)/shard_map/ppermute | solution.py:329
  47.1 1.6 %border_rows.1 = (f32[8,1024]{1,0:T(8,128)}, f32[8,1024]{1,0:T(8,128)}) custom-call(f32[1,8]{1,0:T(1,128)} %table.3, s32[1,128,1024]{2,1,0:T(8,128)} %cb.1, f32[1,128,1024]{2,1,0:T(8,128)} %current.3, s32[1,128,1024]{2,1,0:T(8,128)} %pb.1, s32[128,1024]{1,0:T(8,128)} %vias.3, s32[1,128,1024]{2,1,0:T(8,128)} %cb.1, f32[1,128,1024]{2,1,0:T(8,128)} %current.3, ...), custom_call_target="tpu_custom_call" | custom-call | tf_op jit(solution)/shard_map/border_rows/pallas_call | solution.py:311
  48.7 1.3 %collective-permute-start.1 = (f32[8,1024]{1,0:T(8,128)}, f32[8,1024]{1,0:T(8,128)S(1)}, u32[]{:S(2)}, u32[]{:S(2)}) collective-permute-start(f32[8,1024]{1,0:T(8,128)} %get-tuple-element.13), channel_id=1, source_target_pairs={{0,8},{8,16},{16,24},{24,32},{32,40},{40,48},{48,56},{56,64},{64,7... | collective-permute-start | bytes 98312 | tf_op jit(solution)/shard_map/ppermute | solution.py:319
  50.0 1.3 %collective-permute-start.2 = (f32[8,1024]{1,0:T(8,128)}, f32[8,1024]{1,0:T(8,128)S(1)}, u32[]{:S(2)}, u32[]{:S(2)}) collective-permute-start(f32[8,1024]{1,0:T(8,128)} %get-tuple-element.14), channel_id=1, source_target_pairs={{8,0},{16,8},{24,16},{32,24},{40,32},{48,40},{56,48},{64,56},{72,6... | collective-permute-start | bytes 98312 | tf_op jit(solution)/shard_map/ppermute | solution.py:320
  51.3 0.0 collective-permute-done.1.top
  51.3 0.0 copy-start.1
  51.3 3.6 %collective-permute-done.2.bottom = f32[8,1024]{1,0:T(8,128)S(1)} collective-permute-done((f32[8,1024]{1,0:T(8,128)}, f32[8,1024]{1,0:T(8,128)S(1)}, u32[]{:S(2)}, u32[]{:S(2)}) %collective-permute-start.2) | collective-permute-done | bytes 32800 | tf_op jit(solution)/shard_map/ppermute | solution.py:320
  54.9 0.0 copy-start.2
  54.9 3.1 %collective-permute-start.3 = (f32[16,1024]{1,0:T(8,128)S(1)}, f32[16,1024]{1,0:T(8,128)S(1)}, u32[]{:S(2)}, u32[]{:S(2)}) collective-permute-start(f32[16,1024]{1,0:T(8,128)S(1)} %pad_maximum_fusion), channel_id=1, source_target_pairs={{0,1},{1,0},{2,3},{3,2},{4,5},{5,4},{6,7},{7,6},{8,9},{9,8},{10,11... | collective-permute-start | bytes 196616 | tf_op jit(solution)/shard_map/ppermute | solution.py:331
  58.0 0.7 pad_add_fusion.place
  58.7 0.0 copy-done.1
  58.7 0.0 copy-done.2
  58.7 1.6 %border_columns.1 = f32[8,8,256]{2,1,0:T(8,128)} custom-call(s32[2]{0:T(128)} %pad_add_fusion.place, f32[8,1024]{1,0:T(8,128)} %copy-done.1, f32[8,1024]{1,0:T(8,128)} %copy-done.2, f32[16,128]{1,0:T(8,128)} %get-tuple-element.15.strips), custom_call_target="tpu_custom_call" | custom-call | tf_op jit(solution)/shard_map/border_columns/pallas_call | solution.py:332
  60.3 8.9 %all_to_all.10.recv = f32[8,8,256]{2,1,0:T(8,128)} all-to-all(f32[8,8,256]{2,1,0:T(8,128)} %border_columns.1), channel_id=1, replica_groups=mesh['scen'=2,'row'=32,'col'=4,'layer'=2] {'col','layer'}, dimensions={0} | all-to-all | bytes 131072 | tf_op jit(solution)/shard_map/all_to_all | solution.py:339
  69.1 0.0 collective-permute-done.3.frames
  69.1 0.0 copy-start.3
  69.1 0.0 collective-permute-done.other
  69.1 0.6 copy-done.3
  69.8 0.0 copy-start
  69.8 1.2 copy-done
  70.9 13.1 %grid.1 = (f32[128,1024]{1,0:T(8,128)}, f32[128,1024]{1,0:T(8,128)}, f32[128,1024]{1,0:T(8,128)}, f32[128,1024]{1,0:T(8,128)}, f32[128,1,128]{2,1,0:T(1,128)}) custom-call(s32[2]{0:T(128)} %pad_add_fusion.place, f32[3,128,1024]{2,1,0:T(8,128)} %get-tuple-element.12.own, f32[3,128,1024]{2,1,0:T(8,128)} %copy-done, s32[128,1024]{1,0:T(8,128)} %vias.3, ...), custom_call_target="tpu_custom_call" | custom-call | tf_op jit(solution)/shard_map/grid/pallas_call | solution.py:343
  84.0 35.3 %all_to_all.11.parts = f32[128,1,128]{2,1,0:T(1,128)} all-to-all(f32[128,1,128]{2,1,0:T(1,128)} %get-tuple-element.16), channel_id=1, replica_groups=mesh['scen'=2,'row'=32,'col'=4,'layer'=2] {'row','col'}, dimensions={0} | all-to-all | bytes 131072 | tf_op jit(solution)/shard_map/all_to_all | solution.py:351
  119.3 4.4 %finish.1 = (f32[1,128,1024]{2,1,0:T(8,128)}, f32[1,128,1024]{2,1,0:T(8,128)}, f32[1,128,1024]{2,1,0:T(8,128)}) custom-call(f32[128,1,128]{2,1,0:T(1,128)} %all_to_all.11.parts, f32[1,128,1024]{2,1,0:T(8,128)} %current.3, f32[128,1024]{1,0:T(8,128)} %get-tuple-element.17.z, f32[128,1024]{1,0:T(8,128)} %get-tuple-element.18.u, ...), custom_call_target="tpu_custom_call" | custom-call | tf_op jit(solution)/shard_map/finish/pallas_call | solution.py:357
  (1 shorter events, 0.0 us)
Async XLA Ops:
  3.7 65.4 %collective-permute-start = (f32[3,128,1024]{2,1,0:T(8,128)}, f32[3,128,1024]{2,1,0:T(8,128)S(1)}, u32[]{:S(2)}, u32[]{:S(2)}) collective-permute-start(f32[3,128,1024]{2,1,0:T(8,128)} %get-tuple-element.12.own), channel_id=1, source_target_pairs={{0,1},{1,0},{2,3},{3,2},{4,5},{5,4},{6,7},{7,6},{8,9},{9,8},{10,11... | collective-permute-start | bytes 4718600 | tf_op jit(solution)/shard_map/ppermute | solution.py:329
  48.7 2.6 %collective-permute-start.1 = (f32[8,1024]{1,0:T(8,128)}, f32[8,1024]{1,0:T(8,128)S(1)}, u32[]{:S(2)}, u32[]{:S(2)}) collective-permute-start(f32[8,1024]{1,0:T(8,128)} %get-tuple-element.13), channel_id=1, source_target_pairs={{0,8},{8,16},{16,24},{24,32},{32,40},{40,48},{48,56},{56,64},{64,7... | collective-permute-start | bytes 98312 | tf_op jit(solution)/shard_map/ppermute | solution.py:319
  50.0 4.9 %collective-permute-start.2 = (f32[8,1024]{1,0:T(8,128)}, f32[8,1024]{1,0:T(8,128)S(1)}, u32[]{:S(2)}, u32[]{:S(2)}) collective-permute-start(f32[8,1024]{1,0:T(8,128)} %get-tuple-element.14), channel_id=1, source_target_pairs={{8,0},{16,8},{24,16},{32,24},{40,32},{48,40},{56,48},{64,56},{72,6... | collective-permute-start | bytes 98312 | tf_op jit(solution)/shard_map/ppermute | solution.py:320
  51.3 7.3 %copy-start.1 = (f32[8,1024]{1,0:T(8,128)}, f32[8,1024]{1,0:T(8,128)S(1)}, u32[]{:S(2)}) copy-start(f32[8,1024]{1,0:T(8,128)S(1)} %collective-permute-done.1.top) | copy-start | bytes 98308
  54.9 3.8 %copy-start.2 = (f32[8,1024]{1,0:T(8,128)}, f32[8,1024]{1,0:T(8,128)S(1)}, u32[]{:S(2)}) copy-start(f32[8,1024]{1,0:T(8,128)S(1)} %collective-permute-done.2.bottom) | copy-start | bytes 98308
  54.9 14.2 %collective-permute-start.3 = (f32[16,1024]{1,0:T(8,128)S(1)}, f32[16,1024]{1,0:T(8,128)S(1)}, u32[]{:S(2)}, u32[]{:S(2)}) collective-permute-start(f32[16,1024]{1,0:T(8,128)S(1)} %pad_maximum_fusion), channel_id=1, source_target_pairs={{0,1},{1,0},{2,3},{3,2},{4,5},{5,4},{6,7},{7,6},{8,9},{9,8},{10,11... | collective-permute-start | bytes 196616 | tf_op jit(solution)/shard_map/ppermute | solution.py:331
  69.1 0.6 copy-start.3
  69.8 1.2 copy-start

commit v3 on v2

v3 whole, which is shorter than its diff:
```python
import jax
import jax.numpy as jnp
from jax import lax
from jax.experimental import pallas as pl
from jax.experimental.pallas import tpu as pltpu
from jax.sharding import PartitionSpec as P


via_conductance = 2.0
pad_conductance = 4.0
leakage = 0.05

SUB = 8
LANE = 128


def lanes_of(shape):
    return lax.broadcasted_iota(jnp.int32, shape, len(shape) - 1)


def rows_of(shape):
    return lax.broadcasted_iota(jnp.int32, shape, len(shape) - 2)


def turned(value, shift, axis):
    size = value.shape[axis]
    return pltpu.roll(value, shift % size, axis) if shift % size else value


def half_conductance(classes, table):
    cond = jnp.zeros(classes.shape, jnp.float32)
    for klass in range(table.shape[1]):
        cond = jnp.where(classes == klass, 0.5 * table[0, klass], cond)
    return cond


def pad_term(pads):
    return pad_conductance * pads.astype(jnp.float32) + leakage


def via_term(vias):
    return via_conductance * vias.astype(jnp.float32)


def border_rows(table, top, bottom):
    out = []
    for blocks, shifts, far in ((top, (0, 3, 5, 7), 1), (bottom, (3, 5, 7, 0), SUB - 2)):
        classes, current, pads, vias = blocks
        row = rows_of(current.shape)
        cond = half_conductance(classes, table)
        coupling = via_term(vias)
        own = pad_term(pads)
        own = jnp.where(row == far, own + coupling, own)
        parts = [turned(v, s, 0) for v, s in zip((cond, current, own, coupling), shifts)]
        out.append(
            jnp.where(row < 3, parts[0], jnp.where(row < 5, parts[1], jnp.where(row < 7, parts[2], parts[3])))
        )
    return out


def rows_kernel(table, ct, rt, pt, vt, cb, rb, pb, vb, up, down):
    up[...], down[...] = border_rows(
        table, (ct[0], rt[0], pt[0], vt[...]), (cb[0], rb[0], pb[0], vb[...])
    )


def border_columns(low, high):
    lane = lanes_of(low[0].shape)
    out = None
    for blocks, shifts, far, start in ((high, (3, 5, 7, 8), LANE - 2, 0), (low, (8, 11, 13, 15), 1, 8)):
        cond, current, own, coupling = blocks
        own = jnp.where(lane == far, own + coupling, own)
        parts = [turned(v, s, 1) for v, s in zip((cond, current, own, coupling), shifts)]
        at = lane - start
        side = jnp.where(at < 3, parts[0], jnp.where(at < 5, parts[1], jnp.where(at < 7, parts[2], parts[3])))
        out = side if out is None else jnp.where(lane < start, out, side)
    return out


def tile_kernel(table, classes, current, pads, vias, bulk, coup, strips):
    rows, width = vias.shape

    def strip(s, carry):
        at = pl.ds(pl.multiple_of(s * SUB, SUB), SUB)
        bulk[0, at, :] = half_conductance(classes[0, at, :], table)
        bulk[1, at, :] = current[0, at, :]
        bulk[2, at, :] = pad_term(pads[0, at, :])
        coup[at, :] = via_term(vias[at, :])
        return carry

    lax.fori_loop(0, rows // SUB, strip, 0)
    sides = [
        (bulk[0, :, at], bulk[1, :, at], bulk[2, :, at], coup[:, at])
        for at in (slice(0, LANE), slice(width - LANE, width))
    ]
    strips[...] = border_columns(*sides).T[: 2 * SUB]


def spread_rows(message, below):
    shifts, firsts = ((0, 5, 3, 1), (0, 0, 0, 0)) if below else ((5, 3, 1, 0), (5, 6, 6, 7))
    counts = (3, 2, 2, 1)
    row = rows_of(message.shape)
    return [
        jnp.where((row >= f) & (row < f + n), turned(message, s, 0), 0.0)
        for s, f, n in zip(shifts, firsts, counts)
    ]


def send_kernel(top, bottom, strips, send):
    width = top.shape[1]
    c = lax.axis_index("col")
    blocks = []
    for at in (slice(0, LANE), slice(width - LANE, width)):
        above = spread_rows(top[:, at], False)
        under = spread_rows(bottom[:, at], True)
        blocks.append([jnp.concatenate([a, b], axis=0) for a, b in zip(above, under)])
    around = border_columns(*blocks)
    around = jnp.concatenate([around, jnp.zeros((LANE - 2 * SUB, LANE), jnp.float32)], axis=0).T
    high = jnp.concatenate([strips[:SUB], around[:SUB]], axis=1)
    low = jnp.concatenate([strips[SUB:], around[SUB : 2 * SUB]], axis=1)
    for k in range(send.shape[0]):
        send[k] = jnp.where(k // 2 > c, high, low)


def side_lanes(left, right):
    fill = jnp.zeros((LANE - 2 * SUB, LANE), jnp.float32)
    both = jnp.concatenate([left, right, fill], axis=0).T
    lane = lanes_of(both.shape)
    out = []
    for first, before, after in ((0, 3, 3), (3, 2, 2), (5, 2, 2), (7, 1, 1)):
        low = turned(both, LANE - before - first, 1)
        high = turned(both, -SUB - first, 1)
        out.append(jnp.where(lane >= LANE - before, low, jnp.where(lane < after, high, 0.0)))
    return out


def grid_kernel(
    own, other, coup, top, bottom, frames, recv,
    z_out, u_out, w_out, v_out, sums,
    side, rim, eh, ev, inv, z, u, flux,
):
    rows, width = coup.shape
    strips = rows // SUB
    wide = width + LANE
    columns = recv.shape[0] // 2
    c, place = lax.axis_index("col"), lax.axis_index("layer")

    for layer in range(2):
        mine = place if layer == 0 else 1 - place
        left = recv[jnp.maximum(2 * (c - 1) + mine, 0)]
        left = jnp.where(c > 0, left, 0.0)
        right = recv[jnp.minimum(2 * (c + 1) + mine, 2 * columns - 1)]
        right = jnp.where(c < columns - 1, right, 0.0)
        beside = side_lanes(left[:, :LANE], right[:, :LANE])
        corner = side_lanes(left[:, LANE:], right[:, LANE:])
        above = spread_rows(top[...] if layer == 0 else frames[:SUB], False)
        under = spread_rows(bottom[...] if layer == 0 else frames[SUB:], True)
        for k in range(4 - layer):
            side[4 * layer + k] = beside[k]
            rim[4 * layer + k, 0, :, :width] = above[k]
            rim[4 * layer + k, 1, :, :width] = under[k]
            rim[4 * layer + k, 0, :, width:] = corner[k][:SUB]
            rim[4 * layer + k, 1, :, width:] = corner[k][SUB : 2 * SUB]

    row = rows_of((SUB, wide))
    first, last = row == 0, row == SUB - 1

    def at(s):
        return pl.ds(pl.multiple_of((s + 1) * SUB, SUB), SUB)

    def tile(s):
        return pl.ds(pl.multiple_of((s - 1) * SUB, SUB), SUB)

    def given(k, layer, s):
        if isinstance(s, int) and not 1 <= s <= strips:
            return rim[4 * layer + k, 0 if s == 0 else 1]
        source = coup[tile(s), :] if k == 3 else (other if layer else own)[k, tile(s), :]
        return jnp.concatenate([source, side[4 * layer + k, tile(s), :]], axis=1)

    def after(value):
        return turned(value, -1, 1)

    def before(value):
        return turned(value, 1, 1)

    def below(value, following):
        return turned(jnp.where(first, following, value), -1, 0)

    def above_of(value, preceding):
        return turned(jnp.where(last, preceding, value), 1, 0)

    def inside(a, b, edge):
        return jnp.where((a > 0.0) & (b > 0.0), edge, 0.0)

    def beyond(value, fix):
        return jnp.concatenate([value[:, : width - LANE], fix(slice(width - LANE, wide))], axis=1)

    def scale(s):
        static = isinstance(s, int)
        k = given(3, 0, s)
        for layer in range(2):
            c = given(0, layer, s)
            on = after(c)
            h = c + on
            h = beyond(h, lambda l: inside(c[:, l], on[:, l], h[:, l]))
            if static and s == strips + 1:
                v = c + turned(c, -1, 0)
            else:
                under = below(c, given(0, layer, s + 1))
                v = c + under
                if static:
                    v = inside(c, under, v)
            eh[layer, at(s), :] = h
            ev[layer, at(s), :] = v
            diagonal = h + before(h) + v + k + given(2, layer, s)
            if not static or s > 0:
                diagonal = diagonal + above_of(v, ev[layer, at(s - 1), :])
            else:
                diagonal = diagonal + turned(v, 1, 0)
            inverse = 1.0 / diagonal
            if static and not 1 <= s <= strips:
                inverse = jnp.where(c > 0.0, inverse, 0.0)
            else:
                l = slice(width, wide)
                inverse = jnp.concatenate(
                    [inverse[:, :width], jnp.where(c[:, l] > 0.0, inverse[:, l], 0.0)], axis=1
                )
            inv[layer, at(s), :] = inverse
            z[layer, at(s), :] = given(1, layer, s) * inverse

    def loop(body, carry=None):
        def step(s, t):
            found = body(s)
            return None if t is None else tuple(a + b for a, b in zip(t, found))

        return lax.fori_loop(1, strips, step, carry)

    scale(0)
    loop(scale)
    scale(strips)
    scale(strips + 1)

    def folded(value):
        parts = [value[:, i * LANE : (i + 1) * LANE] for i in range(width // LANE)]
        while len(parts) > 1:
            parts = [a + b for a, b in zip(parts[::2], parts[1::2])]
        return parts[0]

    def down_flux(field, s, layer, x):
        fv = ev[layer, at(s), :] * (x - below(x, field[layer, at(s + 1), :]))
        flux[layer] = fv
        return fv

    def image(field, s, layer, x, exchange):
        fh = eh[layer, at(s), :] * (x - after(x))
        previous = flux[layer]
        fv = down_flux(field, s, layer, x)
        return (fh - before(fh)) + (fv - above_of(fv, previous)) + (exchange + given(2, layer, s) * x)

    def second(s):
        x = [z[layer, at(s), :] for layer in range(2)]
        exchange = given(3, 0, s) * (x[0] - x[1])
        w, y = [], []
        for layer in range(2):
            w.append(image(z, s, layer, x[layer], -exchange if layer else exchange))
            y.append(w[layer] * inv[layer, at(s), :])
            u[layer, at(s), :] = y[layer]
        if isinstance(s, int) and not 1 <= s <= strips:
            return None
        z_out[tile(s), :] = x[0][:, :width]
        w_out[tile(s), :] = w[0][:, :width]
        u_out[tile(s), :] = y[0][:, :width]
        energy = folded(sum(given(1, i, s) * x[i] for i in range(2)))
        curve = folded(sum(x[i] * w[i] for i in range(2)))
        cross = folded(sum(w[i] * y[i] for i in range(2)))
        return energy, curve, cross

    zero = jnp.zeros((SUB, LANE), jnp.float32)
    flux[...] = jnp.zeros(flux.shape, jnp.float32)
    second(0)
    totals = loop(second, (zero,) * 3)
    totals = tuple(a + b for a, b in zip(totals, second(strips)))
    second(strips + 1)

    down_flux(u, 0, 0, u[0, at(0), :])

    def third(s):
        x, y = u[0, at(s), :], u[1, at(s), :]
        exchange = given(3, 0, s) * (x - y)
        v = image(u, s, 0, x, exchange)
        v_out[tile(s), :] = v[:, :width]
        dh = y - after(y)
        dv = y - below(y, u[1, at(s + 1), :])
        there = eh[1, at(s), :] * (dh * dh) + ev[1, at(s), :] * (dv * dv)
        there = there + y * (given(2, 1, s) * y - exchange)
        return (folded(x * v + there),)

    (total,) = loop(third, (zero,))
    total = total + third(strips)[0]
    lane = lanes_of((1, LANE))
    line = jnp.zeros((1, LANE), jnp.float32)
    for k, value in enumerate(totals + (total,)):
        line = jnp.where(lane == k, jnp.sum(value, axis=(0, 1), keepdims=True), line)
    sums[...] = jnp.broadcast_to(line[None], sums.shape)


def finish_kernel(parts, fields, z, u, w, v, drop, resid, worst):
    line = jnp.sum(parts[...], axis=0)
    lane = lanes_of(line.shape)
    energy, curve, cross, last = (
        jnp.sum(jnp.where(lane == k, line, 0.0), axis=1, keepdims=True) for k in range(4)
    )
    step = energy / curve
    energy_next = step * step * cross - energy
    ratio = energy_next / energy
    curve_next = curve - 2.0 * step * cross + step * step * last - ratio * ratio * curve
    step_next = energy_next / curve_next
    mixed = step_next * step
    both = step + step_next * (1.0 + ratio)
    part = drop.shape[1]
    at = pl.ds(pl.multiple_of(pl.program_id(0) * part, SUB), part)
    here = z[at, :]
    second_drop = both * here - mixed * u[at, :]
    drop[0] = second_drop
    worst[0] = jnp.maximum(step * here, second_drop)
    resid[0] = fields[1, at, :] - both * w[at, :] + mixed * v[at, :]


def local(current, node_class, class_conductance, pad_mask, via_mask):
    _, rows, width = current.shape
    n_row, n_col = lax.axis_size("row"), lax.axis_size("col")
    up_pairs = [(i, i + 1) for i in range(n_row - 1)]
    down_pairs = [(b, a) for a, b in up_pairs]
    swap = [(0, 1), (1, 0)]
    f32 = jnp.float32
    smem = pl.BlockSpec(memory_space=pltpu.SMEM)
    vmem = pl.BlockSpec(memory_space=pltpu.VMEM)

    def kept(*dims):
        return pltpu.VMEM(dims, f32)

    def here(value):
        return pltpu.with_memory_space_constraint(value, pltpu.VMEM)

    def room(mib):
        return pltpu.CompilerParams(vmem_limit_bytes=mib << 20)

    def ends(index):
        block = pl.BlockSpec((1, SUB, width), lambda i: (0, index, 0))
        return [block] * 3 + [pl.BlockSpec((SUB, width), lambda i: (index, 0))]

    fields = (node_class, current, pad_mask, via_mask)
    far = tuple(pltpu.with_memory_space_constraint(f, pltpu.HBM) for f in fields)
    up, down = pl.pallas_call(
        rows_kernel,
        grid=(1,),
        in_specs=[smem] + ends(0) + ends(rows // SUB - 1),
        out_specs=[vmem] * 2,
        out_shape=[kept(SUB, width)] * 2,
        compiler_params=room(8),
        name="border_rows",
    )(class_conductance, *far, *far)
    top = lax.ppermute(down, "row", up_pairs)
    bottom = lax.ppermute(up, "row", down_pairs)

    bulk, coup, strips = pl.pallas_call(
        tile_kernel,
        in_specs=[smem] + [vmem] * 4,
        out_specs=[vmem] * 3,
        out_shape=[kept(3, rows, width), kept(rows, width), kept(2 * SUB, LANE)],
        compiler_params=room(16),
        name="tile_fields",
    )(class_conductance, *fields)
    other = lax.ppermute(bulk, "layer", swap)

    frames = lax.ppermute(jnp.concatenate([top, bottom], axis=0), "layer", swap)
    top, bottom = here(top), here(bottom)
    send = pl.pallas_call(
        send_kernel,
        in_specs=[vmem] * 3,
        out_specs=vmem,
        out_shape=kept(2 * n_col, SUB, 2 * LANE),
        compiler_params=room(8),
        name="border_columns",
    )(top, bottom, here(strips))
    recv = lax.all_to_all(send, ("col", "layer"), 0, 0, tiled=True)

    wide = width + LANE
    pair = pltpu.VMEM((2, rows + 4 * SUB, wide), f32)
    z, u, w, v, sums = pl.pallas_call(
        grid_kernel,
        in_specs=[vmem] * 7,
        out_specs=[vmem] * 5,
        out_shape=[kept(rows, width)] * 4 + [kept(n_row * n_col, 1, LANE)],
        scratch_shapes=[
            pltpu.VMEM((7, rows, LANE), f32),
            pltpu.VMEM((7, 2, SUB, wide), f32),
        ]
        + [pair] * 5
        + [pltpu.VMEM((2, SUB, wide), f32)],
        compiler_params=room(24),
        name="grid",
    )(here(bulk), here(other), here(coup), top, bottom, here(frames), here(recv))
    parts = lax.all_to_all(sums, ("row", "col"), 0, 0, tiled=True)

    pieces = 4
    deep = pl.BlockSpec((1, rows // pieces, width), lambda i: (0, i, 0))
    return pl.pallas_call(
        finish_kernel,
        grid=(pieces,),
        in_specs=[vmem] * 6,
        out_specs=[deep] * 3,
        out_shape=[jax.ShapeDtypeStruct((1, rows, width), f32)] * 3,
        compiler_params=room(16),
        name="finish",
    )(here(parts), here(bulk), here(z), here(u), here(w), here(v))


def solution(mesh):
    tile = P("layer", ("scen", "row"), "col")
    in_specs = (tile, tile, P("layer", None), tile, P(("scen", "row"), "col"))

    return jax.shard_map(local, mesh=mesh, in_specs=in_specs, out_specs=(tile,) * 3, check_vma=False)
```

time: 126 us -> 118 us (0.937)
  the two profiles are of different devices: /device:TPU:33 before, /device:TPU:40 now
where the time goes in v3:
time: 118 us; the launch traced here: 117 us
  blocking collectives  82.9 us (70%)
  Pallas kernels  13.8 us (12%)
  starting transfers between devices  9.9 us (8%)
  waiting for transfers between devices  5.29 us (4%)
  local copies, waits for them, and re-layouts  4.81 us (4%)
    all_to_all x1, blocking collectives, local(): parts = lax.all_to_all(sums, ('row', 'col'), 0, 0, tiled=True)  72.8 us
    all_to_all x1, blocking collectives, local(): recv = lax.all_to_all(send, ('col', 'layer'), 0, 0, tiled=True)  10.1 us
    pallas_call x1, Pallas kernels, local(): pl.pallas_call(grid_kernel, in_specs=[vmem] * 7, out_specs=[vmem] * 5, ou...  9.07 us
    ppermute x1, waiting for transfers between devices, local(): bottom = lax.ppermute(up, 'row', down_pairs)  5.03 us
    unnamed x10, local copies, waits for them, and re-layouts  4.81 us
    ppermute x1, starting transfers between devices, local(): top = lax.ppermute(down, 'row', up_pairs)  4.71 us
  transfers between devices with their start and end apart: 4, of which 2 were waited for; matrix products, arithmetic and copies ran while one was open for 0% of the time, Pallas kernels for 1%

profile of v3, /device:TPU:40, one launch (start us, length us, event | category | flops | bytes accessed | tf_op | source)
XLA Modules:
  0.0 117.3 jit_solution(11183342991089720379)
XLA Ops:
  0.6 0.0 copy-start
  0.6 1.0 copy-done
  1.7 0.0 copy-start.1
  1.7 1.0 copy-done.1
  2.7 0.0 copy-start.2
  2.7 1.0 copy-done.2
  3.8 0.0 copy-start.3
  3.8 1.0 copy-done.3
  4.8 0.0 copy-start.4
  4.8 0.7 copy-done.4
  5.5 1.3 %tile_fields.1 = (f32[3,128,1024]{2,1,0:T(8,128)S(1)}, f32[128,1024]{1,0:T(8,128)S(1)}, f32[16,128]{1,0:T(8,128)S(1)}) custom-call(f32[1,8]{1,0:T(1,128)S(1)} %copy-done.4, s32[1,128,1024]{2,1,0:T(8,128)S(1)} %copy-done, f32[1,128,1024]{2,1,0:T(8,128)S(1)} %copy-done.1, s32[1,128,1024]{2,1,0:T(8,128)S(1)} %copy-done.2, s32[128,1024]{1,0:T(8,128)S(1)} %copy-done.3), custom_call_target="tpu_custom_call" | custom-call | tf_op jit(solution)/shard_map/tile_fields/pallas_call | solution.py:366
  6.7 1.9 %collective-permute-start = (f32[3,128,1024]{2,1,0:T(8,128)S(1)}, f32[3,128,1024]{2,1,0:T(8,128)S(1)}, u32[]{:S(2)}, u32[]{:S(2)}) collective-permute-start(f32[3,128,1024]{2,1,0:T(8,128)S(1)} %get-tuple-element.13.own.fields), channel_id=1, source_target_pairs={{0,1},{1,0},{2,3},{3,2},{4,5},{5,4},{6,7},{7,6},{8,9},{9,8},{10,11... | collective-permute-start | bytes 4718600 | tf_op jit(solution)/shard_map/ppermute | solution.py:374
  8.7 1.0 border_rows.1
  9.6 4.7 %collective-permute-start.1 = (f32[8,1024]{1,0:T(8,128)S(1)}, f32[8,1024]{1,0:T(8,128)S(1)}, u32[]{:S(2)}, u32[]{:S(2)}) collective-permute-start(f32[8,1024]{1,0:T(8,128)S(1)} %get-tuple-element.15), channel_id=1, source_target_pairs={{0,8},{8,16},{16,24},{24,32},{32,40},{40,48},{48,56},{56,64},{64,7... | collective-permute-start | bytes 98312 | tf_op jit(solution)/shard_map/ppermute | solution.py:363
  14.4 1.3 %collective-permute-start.2 = (f32[8,1024]{1,0:T(8,128)S(1)}, f32[8,1024]{1,0:T(8,128)S(1)}, u32[]{:S(2)}, u32[]{:S(2)}) collective-permute-start(f32[8,1024]{1,0:T(8,128)S(1)} %get-tuple-element.16), channel_id=1, source_target_pairs={{8,0},{16,8},{24,16},{32,24},{40,32},{48,40},{56,48},{64,56},{72,6... | collective-permute-start | bytes 98312 | tf_op jit(solution)/shard_map/ppermute | solution.py:364
  15.7 0.3 collective-permute-done.1.top
  15.9 5.0 %collective-permute-done.2.bottom = f32[8,1024]{1,0:T(8,128)S(1)} collective-permute-done((f32[8,1024]{1,0:T(8,128)S(1)}, f32[8,1024]{1,0:T(8,128)S(1)}, u32[]{:S(2)}, u32[]{:S(2)}) %collective-permute-start.2) | collective-permute-done | bytes 32800 | tf_op jit(solution)/shard_map/ppermute | solution.py:364
  21.0 1.9 %collective-permute-start.3 = (f32[16,1024]{1,0:T(8,128)S(1)}, f32[16,1024]{1,0:T(8,128)S(1)}, u32[]{:S(2)}, u32[]{:S(2)}) collective-permute-start(f32[16,1024]{1,0:T(8,128)S(1)} %pad_maximum_fusion), channel_id=1, source_target_pairs={{0,1},{1,0},{2,3},{3,2},{4,5},{5,4},{6,7},{7,6},{8,9},{9,8},{10,11... | collective-permute-start | bytes 196616 | tf_op jit(solution)/shard_map/ppermute | solution.py:376
  22.9 0.2 border_columns.1
  23.1 10.1 %all_to_all.10.recv = f32[8,8,256]{2,1,0:T(8,128)S(1)} all-to-all(f32[8,8,256]{2,1,0:T(8,128)S(1)} %border_columns.1), channel_id=1, replica_groups=mesh['scen'=2,'row'=32,'col'=4,'layer'=2] {'col','layer'}, dimensions={0} | all-to-all | bytes 131072 | tf_op jit(solution)/shard_map/all_to_all | solution.py:386
  33.2 0.0 collective-permute-done.3.frames
  33.2 0.0 collective-permute-done.other
  33.2 9.1 %grid.1 = (f32[128,1024]{1,0:T(8,128)S(1)}, f32[128,1024]{1,0:T(8,128)S(1)}, f32[128,1024]{1,0:T(8,128)S(1)}, f32[128,1024]{1,0:T(8,128)S(1)}, f32[128,1,128]{2,1,0:T(1,128)S(1)}) custom-call(f32[3,128,1024]{2,1,0:T(8,128)S(1)} %get-tuple-element.13.own.fields, f32[3,128,1024]{2,1,0:T(8,128)S(1)} %collective-permute-done.other, ...), custom_call_target="tpu_custom_call" | custom-call | tf_op jit(solution)/shard_map/grid/pallas_call | solution.py:390
  42.3 72.8 %all_to_all.11.parts = f32[128,1,128]{2,1,0:T(1,128)S(1)} all-to-all(f32[128,1,128]{2,1,0:T(1,128)S(1)} %get-tuple-element.18), channel_id=1, replica_groups=mesh['scen'=2,'row'=32,'col'=4,'layer'=2] {'row','col'}, dimensions={0} | all-to-all | bytes 131072 | tf_op jit(solution)/shard_map/all_to_all | solution.py:404
  115.0 2.3 %finish.1 = (f32[1,128,1024]{2,1,0:T(8,128)}, f32[1,128,1024]{2,1,0:T(8,128)}, f32[1,128,1024]{2,1,0:T(8,128)}) custom-call(f32[128,1,128]{2,1,0:T(1,128)S(1)} %all_to_all.11.parts, f32[3,128,1024]{2,1,0:T(8,128)S(1)} %get-tuple-element.13.own.fields, f32[128,1024]{1,0:T(8,128)S(1)} %get-tuple-element.19.z, f32[128,1024]{1,0:T(8,128)S(1)} %get-tuple-element.20.u, ...), custom_call_target="tpu_custom_call" | custom-call | tf_op jit(solution)/shard_map/finish/pallas_call | solution.py:408
  (1 shorter events, 0.0 us)
Async XLA Ops:
  0.6 1.0 copy-start
  1.7 1.0 copy-start.1
  2.7 1.0 copy-start.2
  3.8 1.0 copy-start.3
  4.8 0.7 copy-start.4
  6.7 26.5 %collective-permute-start = (f32[3,128,1024]{2,1,0:T(8,128)S(1)}, f32[3,128,1024]{2,1,0:T(8,128)S(1)}, u32[]{:S(2)}, u32[]{:S(2)}) collective-permute-start(f32[3,128,1024]{2,1,0:T(8,128)S(1)} %get-tuple-element.13.own.fields), channel_id=1, source_target_pairs={{0,1},{1,0},{2,3},{3,2},{4,5},{5,4},{6,7},{7,6},{8,9},{9,8},{10,11... | collective-permute-start | bytes 4718600 | tf_op jit(solution)/shard_map/ppermute | solution.py:374
  9.6 6.3 %collective-permute-start.1 = (f32[8,1024]{1,0:T(8,128)S(1)}, f32[8,1024]{1,0:T(8,128)S(1)}, u32[]{:S(2)}, u32[]{:S(2)}) collective-permute-start(f32[8,1024]{1,0:T(8,128)S(1)} %get-tuple-element.15), channel_id=1, source_target_pairs={{0,8},{8,16},{16,24},{24,32},{32,40},{40,48},{48,56},{56,64},{64,7... | collective-permute-start | bytes 98312 | tf_op jit(solution)/shard_map/ppermute | solution.py:363
  14.4 6.6 %collective-permute-start.2 = (f32[8,1024]{1,0:T(8,128)S(1)}, f32[8,1024]{1,0:T(8,128)S(1)}, u32[]{:S(2)}, u32[]{:S(2)}) collective-permute-start(f32[8,1024]{1,0:T(8,128)S(1)} %get-tuple-element.16), channel_id=1, source_target_pairs={{8,0},{16,8},{24,16},{32,24},{40,32},{48,40},{56,48},{64,56},{72,6... | collective-permute-start | bytes 98312 | tf_op jit(solution)/shard_map/ppermute | solution.py:364
  21.0 12.2 %collective-permute-start.3 = (f32[16,1024]{1,0:T(8,128)S(1)}, f32[16,1024]{1,0:T(8,128)S(1)}, u32[]{:S(2)}, u32[]{:S(2)}) collective-permute-start(f32[16,1024]{1,0:T(8,128)S(1)} %pad_maximum_fusion), channel_id=1, source_target_pairs={{0,1},{1,0},{2,3},{3,2},{4,5},{5,4},{6,7},{7,6},{8,9},{9,8},{10,11... | collective-permute-start | bytes 196616 | tf_op jit(solution)/shard_map/ppermute | solution.py:376

commit v4 on v3

--- a/solution.py
+++ b/solution.py
@@ -12,6 +12,7 @@
 
 SUB = 8
 LANE = 128
+TOGETHER = 5
 
 
 def lanes_of(shape):
@@ -79,18 +80,19 @@
 
 def tile_kernel(table, classes, current, pads, vias, bulk, coup, strips):
     rows, width = vias.shape
+    fields = [bulk.at[pl.ds(k * rows, rows)] for k in range(3)]
 
     def strip(s, carry):
         at = pl.ds(pl.multiple_of(s * SUB, SUB), SUB)
-        bulk[0, at, :] = half_conductance(classes[0, at, :], table)
-        bulk[1, at, :] = current[0, at, :]
-        bulk[2, at, :] = pad_term(pads[0, at, :])
+        fields[0][at, :] = half_conductance(classes[0, at, :], table)
+        fields[1][at, :] = current[0, at, :]
+        fields[2][at, :] = pad_term(pads[0, at, :])
         coup[at, :] = via_term(vias[at, :])
         return carry
 
     lax.fori_loop(0, rows // SUB, strip, 0)
     sides = [
-        (bulk[0, :, at], bulk[1, :, at], bulk[2, :, at], coup[:, at])
+        tuple(field[:, at] for field in fields) + (coup[:, at],)
         for at in (slice(0, LANE), slice(width - LANE, width))
     ]
     strips[...] = border_columns(*sides).T[: 2 * SUB]
@@ -135,9 +137,9 @@
 
 
 def grid_kernel(
-    own, other, coup, top, bottom, frames, recv,
+    own, other, coup, recv,
     z_out, u_out, w_out, v_out, sums,
-    side, rim, eh, ev, inv, z, u, flux,
+    side, rim, eh, el, ev, inv, z, u,
 ):
     rows, width = coup.shape
     strips = rows // SUB
@@ -153,8 +155,9 @@
         right = jnp.where(c < columns - 1, right, 0.0)
         beside = side_lanes(left[:, :LANE], right[:, :LANE])
         corner = side_lanes(left[:, LANE:], right[:, LANE:])
-        above = spread_rows(top[...] if layer == 0 else frames[:SUB], False)
-        under = spread_rows(bottom[...] if layer == 0 else frames[SUB:], True)
+        source = other if layer else own
+        above = spread_rows(source[3 * rows : 3 * rows + SUB], False)
+        under = spread_rows(source[3 * rows + SUB :], True)
         for k in range(4 - layer):
             side[4 * layer + k] = beside[k]
             rim[4 * layer + k, 0, :, :width] = above[k]
@@ -168,13 +171,13 @@
     def at(s):
         return pl.ds(pl.multiple_of((s + 1) * SUB, SUB), SUB)
 
-    def tile(s):
-        return pl.ds(pl.multiple_of((s - 1) * SUB, SUB), SUB)
+    def tile(s, k=0):
+        return pl.ds(pl.multiple_of(k * rows + (s - 1) * SUB, SUB), SUB)
 
     def given(k, layer, s):
         if isinstance(s, int) and not 1 <= s <= strips:
             return rim[4 * layer + k, 0 if s == 0 else 1]
-        source = coup[tile(s), :] if k == 3 else (other if layer else own)[k, tile(s), :]
+        source = coup[tile(s), :] if k == 3 else (other if layer else own)[tile(s, k), :]
         return jnp.concatenate([source, side[4 * layer + k, tile(s), :]], axis=1)
 
     def after(value):
@@ -192,17 +195,26 @@
     def inside(a, b, edge):
         return jnp.where((a > 0.0) & (b > 0.0), edge, 0.0)
 
-    def beyond(value, fix):
-        return jnp.concatenate([value[:, : width - LANE], fix(slice(width - LANE, wide))], axis=1)
-
-    def scale(s):
+    def seam(value, blocks, fix):
+        parts, start = [], 0
+        for k in sorted(blocks):
+            parts += [value[:, start : k * LANE]] if k * LANE > start else []
+            parts.append(fix(slice(k * LANE, (k + 1) * LANE)))
+            start = (k + 1) * LANE
+        return jnp.concatenate(parts + ([value[:, start:]] if start < wide else []), axis=1)
+
+    end = width // LANE
+
+    def scale(s, previous):
         static = isinstance(s, int)
         k = given(3, 0, s)
+        kept = []
         for layer in range(2):
             c = given(0, layer, s)
-            on = after(c)
-            h = c + on
-            h = beyond(h, lambda l: inside(c[:, l], on[:, l], h[:, l]))
+            on, back = after(c), before(c)
+            h, g = c + on, c + back
+            h = seam(h, (end - 1, end), lambda l: inside(c[:, l], on[:, l], h[:, l]))
+            g = seam(g, (0, end), lambda l: inside(c[:, l], back[:, l], g[:, l]))
             if static and s == strips + 1:
                 v = c + turned(c, -1, 0)
             else:
@@ -211,34 +223,38 @@
                 if static:
                     v = inside(c, under, v)
             eh[layer, at(s), :] = h
+            el[layer, at(s), :] = g
             ev[layer, at(s), :] = v
-            diagonal = h + before(h) + v + k + given(2, layer, s)
-            if not static or s > 0:
-                diagonal = diagonal + above_of(v, ev[layer, at(s - 1), :])
-            else:
-                diagonal = diagonal + turned(v, 1, 0)
+            prior = v if previous is None else previous[layer]
+            diagonal = ((h + g) + (v + above_of(v, prior))) + (k + given(2, layer, s))
             inverse = 1.0 / diagonal
             if static and not 1 <= s <= strips:
                 inverse = jnp.where(c > 0.0, inverse, 0.0)
             else:
-                l = slice(width, wide)
-                inverse = jnp.concatenate(
-                    [inverse[:, :width], jnp.where(c[:, l] > 0.0, inverse[:, l], 0.0)], axis=1
-                )
+                inverse = seam(inverse, (end,), lambda l: jnp.where(c[:, l] > 0.0, inverse[:, l], 0.0))
             inv[layer, at(s), :] = inverse
             z[layer, at(s), :] = given(1, layer, s) * inverse
-
-    def loop(body, carry=None):
-        def step(s, t):
-            found = body(s)
-            return None if t is None else tuple(a + b for a, b in zip(t, found))
-
-        return lax.fori_loop(1, strips, step, carry)
-
-    scale(0)
-    loop(scale)
-    scale(strips)
-    scale(strips + 1)
+            kept.append(v)
+        return kept, None
+
+    def loop(body, recall, totals=()):
+        def step(i, totals):
+            s = 1 + i * TOGETHER
+            previous = recall(s - 1)
+            for k in range(TOGETHER):
+                previous, found = body(s + k, previous)
+                totals = tuple(a + b for a, b in zip(totals, found or ()))
+            return totals
+
+        return lax.fori_loop(0, (strips - 1) // TOGETHER, step, totals)
+
+    def edge_above(s):
+        return [ev[layer, at(s), :] for layer in range(2)]
+
+    scale(0, None)
+    loop(scale, edge_above)
+    kept, _ = scale(strips, edge_above(strips - 1))
+    scale(strips + 1, kept)
 
     def folded(value):
         parts = [value[:, i * LANE : (i + 1) * LANE] for i in range(width // LANE)]
@@ -246,57 +262,59 @@
             parts = [a + b for a, b in zip(parts[::2], parts[1::2])]
         return parts[0]
 
-    def down_flux(field, s, layer, x):
-        fv = ev[layer, at(s), :] * (x - below(x, field[layer, at(s + 1), :]))
-        flux[layer] = fv
-        return fv
-
-    def image(field, s, layer, x, exchange):
-        fh = eh[layer, at(s), :] * (x - after(x))
-        previous = flux[layer]
-        fv = down_flux(field, s, layer, x)
-        return (fh - before(fh)) + (fv - above_of(fv, previous)) + (exchange + given(2, layer, s) * x)
-
-    def second(s):
+    def down_flux(field, s, layer):
+        x = field[layer, at(s), :]
+        return ev[layer, at(s), :] * (x - below(x, field[layer, at(s + 1), :]))
+
+    def image(field, s, layer, x, exchange, previous):
+        across = eh[layer, at(s), :] * (x - after(x)) + el[layer, at(s), :] * (x - before(x))
+        fv = down_flux(field, s, layer)
+        return across + (fv - above_of(fv, previous)) + (exchange + given(2, layer, s) * x), fv
+
+    def second(s, previous):
         x = [z[layer, at(s), :] for layer in range(2)]
         exchange = given(3, 0, s) * (x[0] - x[1])
-        w, y = [], []
+        w, y, kept = [], [], []
         for layer in range(2):
-            w.append(image(z, s, layer, x[layer], -exchange if layer else exchange))
-            y.append(w[layer] * inv[layer, at(s), :])
+            found, fv = image(z, s, layer, x[layer], -exchange if layer else exchange, previous[layer])
+            w.append(found)
+            kept.append(fv)
+            y.append(found * inv[layer, at(s), :])
             u[layer, at(s), :] = y[layer]
         if isinstance(s, int) and not 1 <= s <= strips:
-            return None
+            return kept, None
         z_out[tile(s), :] = x[0][:, :width]
         w_out[tile(s), :] = w[0][:, :width]
         u_out[tile(s), :] = y[0][:, :width]
         energy = folded(sum(given(1, i, s) * x[i] for i in range(2)))
         curve = folded(sum(x[i] * w[i] for i in range(2)))
         cross = folded(sum(w[i] * y[i] for i in range(2)))
-        return energy, curve, cross
+        return kept, (energy, curve, cross)
+
+    def flux_above(field):
+        return lambda s: [down_flux(field, s, layer) for layer in range(2)]
 
     zero = jnp.zeros((SUB, LANE), jnp.float32)
-    flux[...] = jnp.zeros(flux.shape, jnp.float32)
-    second(0)
-    totals = loop(second, (zero,) * 3)
-    totals = tuple(a + b for a, b in zip(totals, second(strips)))
-    second(strips + 1)
-
-    down_flux(u, 0, 0, u[0, at(0), :])
-
-    def third(s):
+    nothing = jnp.zeros((SUB, wide), jnp.float32)
+    second(0, [nothing] * 2)
+    totals = loop(second, flux_above(z), (zero,) * 3)
+    kept, found = second(strips, flux_above(z)(strips - 1))
+    totals = tuple(a + b for a, b in zip(totals, found))
+    second(strips + 1, kept)
+
+    def third(s, previous):
         x, y = u[0, at(s), :], u[1, at(s), :]
         exchange = given(3, 0, s) * (x - y)
-        v = image(u, s, 0, x, exchange)
+        v, fv = image(u, s, 0, x, exchange, previous)
         v_out[tile(s), :] = v[:, :width]
         dh = y - after(y)
         dv = y - below(y, u[1, at(s + 1), :])
         there = eh[1, at(s), :] * (dh * dh) + ev[1, at(s), :] * (dv * dv)
         there = there + y * (given(2, 1, s) * y - exchange)
-        return (folded(x * v + there),)
-
-    (total,) = loop(third, (zero,))
-    total = total + third(strips)[0]
+        return fv, (folded(x * v + there),)
+
+    (total,) = loop(third, lambda s: down_flux(u, s, 0), (zero,))
+    total = total + third(strips, down_flux(u, strips - 1, 0))[1][0]
     lane = lanes_of((1, LANE))
     line = jnp.zeros((1, LANE), jnp.float32)
     for k, value in enumerate(totals + (total,)):
@@ -304,26 +322,32 @@
     sums[...] = jnp.broadcast_to(line[None], sums.shape)
 
 
-def finish_kernel(parts, fields, z, u, w, v, drop, resid, worst):
-    line = jnp.sum(parts[...], axis=0)
-    lane = lanes_of(line.shape)
-    energy, curve, cross, last = (
-        jnp.sum(jnp.where(lane == k, line, 0.0), axis=1, keepdims=True) for k in range(4)
-    )
-    step = energy / curve
-    energy_next = step * step * cross - energy
-    ratio = energy_next / energy
-    curve_next = curve - 2.0 * step * cross + step * step * last - ratio * ratio * curve
-    step_next = energy_next / curve_next
-    mixed = step_next * step
-    both = step + step_next * (1.0 + ratio)
-    part = drop.shape[1]
+def finish_kernel(parts, fields, z, u, w, v, drop, resid, worst, steps):
+    rows, part = z.shape[0], drop.shape[1]
+
+    @pl.when(pl.program_id(0) == 0)
+    def _():
+        line = jnp.sum(parts[...], axis=0)
+        lane = lanes_of(line.shape)
+        energy, curve, cross, last = (
+            jnp.sum(jnp.where(lane == k, line, 0.0), axis=1, keepdims=True) for k in range(4)
+        )
+        step = energy / curve
+        energy_next = step * step * cross - energy
+        ratio = energy_next / energy
+        curve_next = curve - 2.0 * step * cross + step * step * last - ratio * ratio * curve
+        step_next = energy_next / curve_next
+        for k, value in enumerate((step, step + step_next * (1.0 + ratio), step_next * step)):
+            steps[k] = jnp.broadcast_to(value, steps.shape[1:])
+
+    step, both, mixed = (steps[k, :1, :1] for k in range(3))
     at = pl.ds(pl.multiple_of(pl.program_id(0) * part, SUB), part)
     here = z[at, :]
     second_drop = both * here - mixed * u[at, :]
     drop[0] = second_drop
     worst[0] = jnp.maximum(step * here, second_drop)
-    resid[0] = fields[1, at, :] - both * w[at, :] + mixed * v[at, :]
+    given = fields[pl.ds(pl.multiple_of(rows + pl.program_id(0) * part, SUB), part), :]
+    resid[0] = given - both * w[at, :] + mixed * v[at, :]
 
 
 def local(current, node_class, class_conductance, pad_mask, via_mask):
@@ -359,7 +383,7 @@
         out_shape=[kept(SUB, width)] * 2,
         compiler_params=room(8),
         name="border_rows",
-    )(class_conductance, *far, *far)
+    )(pltpu.with_memory_space_constraint(class_conductance, pltpu.HBM), *far, *far)
     top = lax.ppermute(down, "row", up_pairs)
     bottom = lax.ppermute(up, "row", down_pairs)
 
@@ -367,14 +391,12 @@
         tile_kernel,
         in_specs=[smem] + [vmem] * 4,
         out_specs=[vmem] * 3,
-        out_shape=[kept(3, rows, width), kept(rows, width), kept(2 * SUB, LANE)],
+        out_shape=[kept(3 * rows + 2 * SUB, width), kept(rows, width), kept(2 * SUB, LANE)],
         compiler_params=room(16),
         name="tile_fields",
     )(class_conductance, *fields)
-    other = lax.ppermute(bulk, "layer", swap)
-
-    frames = lax.ppermute(jnp.concatenate([top, bottom], axis=0), "layer", swap)
-    top, bottom = here(top), here(bottom)
+    bulk = lax.dynamic_update_slice(bulk, top, (3 * rows, 0))
+    bulk = lax.dynamic_update_slice(bulk, bottom, (3 * rows + SUB, 0))
     send = pl.pallas_call(
         send_kernel,
         in_specs=[vmem] * 3,
@@ -382,28 +404,28 @@
         out_shape=kept(2 * n_col, SUB, 2 * LANE),
         compiler_params=room(8),
         name="border_columns",
-    )(top, bottom, here(strips))
+    )(here(top), here(bottom), here(strips))
+    other = lax.ppermute(bulk, "layer", swap)
     recv = lax.all_to_all(send, ("col", "layer"), 0, 0, tiled=True)
 
     wide = width + LANE
     pair = pltpu.VMEM((2, rows + 4 * SUB, wide), f32)
     z, u, w, v, sums = pl.pallas_call(
         grid_kernel,
-        in_specs=[vmem] * 7,
+        in_specs=[vmem] * 4,
         out_specs=[vmem] * 5,
         out_shape=[kept(rows, width)] * 4 + [kept(n_row * n_col, 1, LANE)],
         scratch_shapes=[
             pltpu.VMEM((7, rows, LANE), f32),
             pltpu.VMEM((7, 2, SUB, wide), f32),
         ]
-        + [pair] * 5
-        + [pltpu.VMEM((2, SUB, wide), f32)],
-        compiler_params=room(24),
+        + [pair] * 6,
+        compiler_params=room(28),
         name="grid",
-    )(here(bulk), here(other), here(coup), top, bottom, here(frames), here(recv))
+    )(here(bulk), here(other), here(coup), here(recv))
     parts = lax.all_to_all(sums, ("row", "col"), 0, 0, tiled=True)
 
-    pieces = 4
+    pieces = 2
     deep = pl.BlockSpec((1, rows // pieces, width), lambda i: (0, i, 0))
     return pl.pallas_call(
         finish_kernel,
@@ -411,6 +433,7 @@
         in_specs=[vmem] * 6,
         out_specs=[deep] * 3,
         out_shape=[jax.ShapeDtypeStruct((1, rows, width), f32)] * 3,
+        scratch_shapes=[pltpu.VMEM((3, SUB, LANE), f32)],
         compiler_params=room(16),
         name="finish",
     )(here(parts), here(bulk), here(z), here(u), here(w), here(v))

time: 118 us -> 104 us (0.88)
  Pallas kernels: 13.8 us -> 8.03 us
  local copies, waits for them, and re-layouts: 4.81 us -> 0.03 us
  starting transfers between devices: 9.9 us -> 7.96 us
  waiting for transfers between devices: 5.29 us -> 3.97 us
    pallas_call x1, Pallas kernels: 9.07 us -> 4.06 us  [local(): pl.pallas_call(grid_kernel, in_specs=[vmem] * 4, out_specs=[vmem] * 5, ou...]
    unnamed x10, local copies, waits for them, and re-layouts: 4.81 us -> 0.02 us
    ppermute x1 -> x0, starting transfers between devices: 1.94 us -> none  [local(): frames = lax.ppermute(jnp.concatenate([top, bottom], axis=0), 'layer', swap)]
  transfers between devices with their start and end apart: 4 -> 3, of which waited for: 2 -> 1; matrix products, arithmetic and copies ran while one was open for 0% -> 0% of each run, Pallas kernels for 1% -> 1%
where the time goes in v4:
time: 104 us
  blocking collectives  82.9 us (80%)
  Pallas kernels  8.03 us (8%)
  starting transfers between devices  7.96 us (8%)
  waiting for transfers between devices  3.97 us (4%)
    all_to_all x1, blocking collectives, local(): parts = lax.all_to_all(sums, ('row', 'col'), 0, 0, tiled=True)  72.8 us
    all_to_all x1, blocking collectives, local(): recv = lax.all_to_all(send, ('col', 'layer'), 0, 0, tiled=True)  10.1 us
    ppermute x1, starting transfers between devices, local(): top = lax.ppermute(down, 'row', up_pairs)  4.71 us
    pallas_call x1, Pallas kernels, local(): pl.pallas_call(grid_kernel, in_specs=[vmem] * 4, out_specs=[vmem] * 5, ou...  4.06 us
    ppermute x1, waiting for transfers between devices, local(): bottom = lax.ppermute(up, 'row', down_pairs)  3.97 us
  transfers between devices with their start and end apart: 3, of which 1 were waited for; matrix products, arithmetic and copies ran while one was open for 0% of the time, Pallas kernels for 1%

profile of v4, /device:TPU:40, one launch (start us, length us, event | category | flops | bytes accessed | tf_op | source)
XLA Modules:
  0.0 103.6 jit_solution(1691737769472948969)
XLA Ops:
  0.6 0.0 copy-start.3
  0.6 0.0 copy-start.2
  0.7 0.0 copy-start.4
  0.7 0.0 copy-start
  0.7 0.0 copy-start.1
  0.7 1.1 %border_rows.1 = (f32[8,1024]{1,0:T(8,128)S(1)}, f32[8,1024]{1,0:T(8,128)S(1)}) custom-call(f32[1,8]{1,0:T(1,128)} %table.3, s32[1,128,1024]{2,1,0:T(8,128)} %cb.1, f32[1,128,1024]{2,1,0:T(8,128)} %rb.1, s32[1,128,1024]{2,1,0:T(8,128)} %pb.1, s32[128,1024]{1,0:T(8,128)} %vb.1, s32[1,128,1024]{2,1,0:T(8,128)} %cb.1, f32[1,128,1024]{2,1,0:T(8,128)} %rb.1, ...), custom_call_target="tpu_custom_call" | custom-call | tf_op jit(solution)/shard_map/border_rows/pallas_call | solution.py:378
  1.8 4.7 %collective-permute-start = (f32[8,1024]{1,0:T(8,128)S(1)}, f32[8,1024]{1,0:T(8,128)S(1)}, u32[]{:S(2)}, u32[]{:S(2)}) collective-permute-start(f32[8,1024]{1,0:T(8,128)S(1)} %get-tuple-element.14), channel_id=1, source_target_pairs={{0,8},{8,16},{16,24},{24,32},{32,40},{40,48},{48,56},{56,64},{64,7... | collective-permute-start | bytes 98312 | tf_op jit(solution)/shard_map/ppermute | solution.py:387
  6.5 1.3 %collective-permute-start.1 = (f32[8,1024]{1,0:T(8,128)S(1)}, f32[8,1024]{1,0:T(8,128)S(1)}, u32[]{:S(2)}, u32[]{:S(2)}) collective-permute-start(f32[8,1024]{1,0:T(8,128)S(1)} %get-tuple-element.15), channel_id=1, source_target_pairs={{8,0},{16,8},{24,16},{32,24},{40,32},{48,40},{56,48},{64,56},{72,6... | collective-permute-start | bytes 98312 | tf_op jit(solution)/shard_map/ppermute | solution.py:388
  7.8 0.0 copy-done.3
  7.8 0.0 copy-done.2
  7.8 0.0 copy-done.4
  7.8 0.0 copy-done
  7.9 0.0 copy-done.1
  7.9 1.3 %tile_fields.1 = (f32[400,1024]{1,0:T(8,128)S(1)}, f32[128,1024]{1,0:T(8,128)S(1)}, f32[16,128]{1,0:T(8,128)S(1)}) custom-call(f32[1,8]{1,0:T(1,128)S(1)} %copy-done.4, s32[1,128,1024]{2,1,0:T(8,128)S(1)} %copy-done, f32[1,128,1024]{2,1,0:T(8,128)S(1)} %copy-done.1, s32[1,128,1024]{2,1,0:T(8,128)S(1)} %copy-done.2, s32[128,1024]{1,0:T(8,128)S(1)} %copy-done.3), custom_call_target="tpu_custom_call" | custom-call | tf_op jit(solution)/shard_map/tile_fields/pallas_call | solution.py:390
  9.1 0.0 collective-permute-done.top
  9.1 4.0 %collective-permute-done.1.bottom = f32[8,1024]{1,0:T(8,128)S(1)} collective-permute-done((f32[8,1024]{1,0:T(8,128)S(1)}, f32[8,1024]{1,0:T(8,128)S(1)}, u32[]{:S(2)}, u32[]{:S(2)}) %collective-permute-start.1) | collective-permute-done | bytes 32800 | tf_op jit(solution)/shard_map/ppermute | solution.py:388
  13.1 1.9 %collective-permute-start.2 = (f32[400,1024]{1,0:T(8,128)S(1)}, f32[400,1024]{1,0:T(8,128)S(1)}, u32[]{:S(2)}, u32[]{:S(2)}) collective-permute-start(f32[400,1024]{1,0:T(8,128)S(1)} %constant_dynamic-update-slice_fusion.own.fields), channel_id=1, source_target_pairs={{0,1},{1,0},{2,3},{3,2},{4,5},{5,4},{6,7},{7,6},{8,9},{9,8},{10,11... | collective-permute-start | bytes 4915208 | tf_op jit(solution)/shard_map/ppermute | solution.py:408
  15.1 0.2 border_columns.1
  15.2 10.1 %all_to_all.10.recv = f32[8,8,256]{2,1,0:T(8,128)S(1)} all-to-all(f32[8,8,256]{2,1,0:T(8,128)S(1)} %border_columns.1), channel_id=1, replica_groups=mesh['scen'=2,'row'=32,'col'=4,'layer'=2] {'col','layer'}, dimensions={0} | all-to-all | bytes 131072 | tf_op jit(solution)/shard_map/all_to_all | solution.py:409
  25.3 0.0 collective-permute-done.2.other
  25.3 4.1 %grid.1 = (f32[128,1024]{1,0:T(8,128)S(1)}, f32[128,1024]{1,0:T(8,128)S(1)}, f32[128,1024]{1,0:T(8,128)S(1)}, f32[128,1024]{1,0:T(8,128)S(1)}, f32[128,1,128]{2,1,0:T(1,128)S(1)}) custom-call(f32[400,1024]{1,0:T(8,128)S(1)} %constant_dynamic-update-slice_fusion.own.fields, f32[400,1024]{1,0:T(8,128)S(1)} %collective-permute-done.2.other, ...), custom_call_target="tpu_custom_call" | custom-call | tf_op jit(solution)/shard_map/grid/pallas_call | solution.py:413
  29.4 72.8 %all_to_all.11.parts = f32[128,1,128]{2,1,0:T(1,128)S(1)} all-to-all(f32[128,1,128]{2,1,0:T(1,128)S(1)} %get-tuple-element.18), channel_id=1, replica_groups=mesh['scen'=2,'row'=32,'col'=4,'layer'=2] {'row','col'}, dimensions={0} | all-to-all | bytes 131072 | tf_op jit(solution)/shard_map/all_to_all | solution.py:426
  102.2 1.5 %finish.1 = (f32[1,128,1024]{2,1,0:T(8,128)}, f32[1,128,1024]{2,1,0:T(8,128)}, f32[1,128,1024]{2,1,0:T(8,128)}) custom-call(f32[128,1,128]{2,1,0:T(1,128)S(1)} %all_to_all.11.parts, f32[400,1024]{1,0:T(8,128)S(1)} %constant_dynamic-update-slice_fusion.own.fields, f32[128,1024]{1,0:T(8,128)S(1)} %get-tuple-element.19.z, f32[128,1024]{1,0:T(8,128)S(1)} %get-tuple-element.20.u, ...), custom_call_target="tpu_custom_call" | custom-call | tf_op jit(solution)/shard_map/finish/pallas_call | solution.py:430
  (2 shorter events, 0.0 us)
Async XLA Ops:
  0.6 7.2 %copy-start.3 = (s32[128,1024]{1,0:T(8,128)S(1)}, s32[128,1024]{1,0:T(8,128)}, u32[]{:S(2)}) copy-start(s32[128,1024]{1,0:T(8,128)} %vb.1) | copy-start | bytes 1572868
  0.6 7.2 %copy-start.2 = (s32[1,128,1024]{2,1,0:T(8,128)S(1)}, s32[1,128,1024]{2,1,0:T(8,128)}, u32[]{:S(2)}) copy-start(s32[1,128,1024]{2,1,0:T(8,128)} %pb.1) | copy-start | bytes 1572868
  0.7 7.2 %copy-start.4 = (f32[1,8]{1,0:T(1,128)S(1)}, f32[1,8]{1,0:T(1,128)}, u32[]{:S(2)}) copy-start(f32[1,8]{1,0:T(1,128)} %table.3) | copy-start | bytes 100
  0.7 7.2 %copy-start = (s32[1,128,1024]{2,1,0:T(8,128)S(1)}, s32[1,128,1024]{2,1,0:T(8,128)}, u32[]{:S(2)}) copy-start(s32[1,128,1024]{2,1,0:T(8,128)} %cb.1) | copy-start | bytes 1572868
  0.7 7.2 %copy-start.1 = (f32[1,128,1024]{2,1,0:T(8,128)S(1)}, f32[1,128,1024]{2,1,0:T(8,128)}, u32[]{:S(2)}) copy-start(f32[1,128,1024]{2,1,0:T(8,128)} %rb.1) | copy-start | bytes 1572868
  1.8 7.3 %collective-permute-start = (f32[8,1024]{1,0:T(8,128)S(1)}, f32[8,1024]{1,0:T(8,128)S(1)}, u32[]{:S(2)}, u32[]{:S(2)}) collective-permute-start(f32[8,1024]{1,0:T(8,128)S(1)} %get-tuple-element.14), channel_id=1, source_target_pairs={{0,8},{8,16},{16,24},{24,32},{32,40},{40,48},{48,56},{56,64},{64,7... | collective-permute-start | bytes 98312 | tf_op jit(solution)/shard_map/ppermute | solution.py:387
  6.5 6.6 %collective-permute-start.1 = (f32[8,1024]{1,0:T(8,128)S(1)}, f32[8,1024]{1,0:T(8,128)S(1)}, u32[]{:S(2)}, u32[]{:S(2)}) collective-permute-start(f32[8,1024]{1,0:T(8,128)S(1)} %get-tuple-element.15), channel_id=1, source_target_pairs={{8,0},{16,8},{24,16},{32,24},{40,32},{48,40},{56,48},{64,56},{72,6... | collective-permute-start | bytes 98312 | tf_op jit(solution)/shard_map/ppermute | solution.py:388
  13.1 12.2 %collective-permute-start.2 = (f32[400,1024]{1,0:T(8,128)S(1)}, f32[400,1024]{1,0:T(8,128)S(1)}, u32[]{:S(2)}, u32[]{:S(2)}) collective-permute-start(f32[400,1024]{1,0:T(8,128)S(1)} %constant_dynamic-update-slice_fusion.own.fields), channel_id=1, source_target_pairs={{0,1},{1,0},{2,3},{3,2},{4,5},{5,4},{6,7},{7,6},{8,9},{9,8},{10,11... | collective-permute-start | bytes 4915208 | tf_op jit(solution)/shard_map/ppermute | solution.py:408

commit v5 on v4

--- a/solution.py
+++ b/solution.py
@@ -12,7 +12,6 @@
 
 SUB = 8
 LANE = 128
-TOGETHER = 5
 
 
 def lanes_of(shape):
@@ -124,9 +123,9 @@
         send[k] = jnp.where(k // 2 > c, high, low)
 
 
-def side_lanes(left, right):
+def side_lanes(left, right, rows=LANE):
     fill = jnp.zeros((LANE - 2 * SUB, LANE), jnp.float32)
-    both = jnp.concatenate([left, right, fill], axis=0).T
+    both = jnp.concatenate([left, right, fill], axis=0).T[:rows]
     lane = lanes_of(both.shape)
     out = []
     for first, before, after in ((0, 3, 3), (3, 2, 2), (5, 2, 2), (7, 1, 1)):
@@ -138,8 +137,8 @@
 
 def grid_kernel(
     own, other, coup, recv,
-    z_out, u_out, w_out, v_out, sums,
-    side, rim, eh, el, ev, inv, z, u,
+    z, u, w_out, v_out, sums,
+    side, rim, eh, el, ev, inv,
 ):
     rows, width = coup.shape
     strips = rows // SUB
@@ -154,7 +153,7 @@
         right = recv[jnp.minimum(2 * (c + 1) + mine, 2 * columns - 1)]
         right = jnp.where(c < columns - 1, right, 0.0)
         beside = side_lanes(left[:, :LANE], right[:, :LANE])
-        corner = side_lanes(left[:, LANE:], right[:, LANE:])
+        corner = side_lanes(left[:, LANE:], right[:, LANE:], 2 * SUB)
         source = other if layer else own
         above = spread_rows(source[3 * rows : 3 * rows + SUB], False)
         under = spread_rows(source[3 * rows + SUB :], True)
@@ -163,19 +162,19 @@
             rim[4 * layer + k, 0, :, :width] = above[k]
             rim[4 * layer + k, 1, :, :width] = under[k]
             rim[4 * layer + k, 0, :, width:] = corner[k][:SUB]
-            rim[4 * layer + k, 1, :, width:] = corner[k][SUB : 2 * SUB]
+            rim[4 * layer + k, 1, :, width:] = corner[k][SUB:]
 
     row = rows_of((SUB, wide))
     first, last = row == 0, row == SUB - 1
 
     def at(s):
-        return pl.ds(pl.multiple_of((s + 1) * SUB, SUB), SUB)
+        return pl.ds((s + 1) * SUB, SUB)
 
     def tile(s, k=0):
-        return pl.ds(pl.multiple_of(k * rows + (s - 1) * SUB, SUB), SUB)
+        return pl.ds(k * rows + (s - 1) * SUB, SUB)
 
     def given(k, layer, s):
-        if isinstance(s, int) and not 1 <= s <= strips:
+        if not 1 <= s <= strips:
             return rim[4 * layer + k, 0 if s == 0 else 1]
         source = coup[tile(s), :] if k == 3 else (other if layer else own)[tile(s, k), :]
         return jnp.concatenate([source, side[4 * layer + k, tile(s), :]], axis=1)
@@ -206,7 +205,6 @@
     end = width // LANE
 
     def scale(s, previous):
-        static = isinstance(s, int)
         k = given(3, 0, s)
         kept = []
         for layer in range(2):
@@ -215,12 +213,12 @@
             h, g = c + on, c + back
             h = seam(h, (end - 1, end), lambda l: inside(c[:, l], on[:, l], h[:, l]))
             g = seam(g, (0, end), lambda l: inside(c[:, l], back[:, l], g[:, l]))
-            if static and s == strips + 1:
+            if s == strips + 1:
                 v = c + turned(c, -1, 0)
             else:
                 under = below(c, given(0, layer, s + 1))
                 v = c + under
-                if static:
+                if s in (0, strips):
                     v = inside(c, under, v)
             eh[layer, at(s), :] = h
             el[layer, at(s), :] = g
@@ -228,33 +226,18 @@
             prior = v if previous is None else previous[layer]
             diagonal = ((h + g) + (v + above_of(v, prior))) + (k + given(2, layer, s))
             inverse = 1.0 / diagonal
-            if static and not 1 <= s <= strips:
+            if not 1 <= s <= strips:
                 inverse = jnp.where(c > 0.0, inverse, 0.0)
             else:
                 inverse = seam(inverse, (end,), lambda l: jnp.where(c[:, l] > 0.0, inverse[:, l], 0.0))
             inv[layer, at(s), :] = inverse
             z[layer, at(s), :] = given(1, layer, s) * inverse
             kept.append(v)
-        return kept, None
-
-    def loop(body, recall, totals=()):
-        def step(i, totals):
-            s = 1 + i * TOGETHER
-            previous = recall(s - 1)
-            for k in range(TOGETHER):
-                previous, found = body(s + k, previous)
-                totals = tuple(a + b for a, b in zip(totals, found or ()))
-            return totals
-
-        return lax.fori_loop(0, (strips - 1) // TOGETHER, step, totals)
-
-    def edge_above(s):
-        return [ev[layer, at(s), :] for layer in range(2)]
-
-    scale(0, None)
-    loop(scale, edge_above)
-    kept, _ = scale(strips, edge_above(strips - 1))
-    scale(strips + 1, kept)
+        return kept
+
+    kept = None
+    for s in range(strips + 2):
+        kept = scale(s, kept)
 
     def folded(value):
         parts = [value[:, i * LANE : (i + 1) * LANE] for i in range(width // LANE)]
@@ -281,26 +264,19 @@
             kept.append(fv)
             y.append(found * inv[layer, at(s), :])
             u[layer, at(s), :] = y[layer]
-        if isinstance(s, int) and not 1 <= s <= strips:
+        if not 1 <= s <= strips:
             return kept, None
-        z_out[tile(s), :] = x[0][:, :width]
         w_out[tile(s), :] = w[0][:, :width]
-        u_out[tile(s), :] = y[0][:, :width]
         energy = folded(sum(given(1, i, s) * x[i] for i in range(2)))
         curve = folded(sum(x[i] * w[i] for i in range(2)))
         cross = folded(sum(w[i] * y[i] for i in range(2)))
         return kept, (energy, curve, cross)
 
-    def flux_above(field):
-        return lambda s: [down_flux(field, s, layer) for layer in range(2)]
-
     zero = jnp.zeros((SUB, LANE), jnp.float32)
-    nothing = jnp.zeros((SUB, wide), jnp.float32)
-    second(0, [nothing] * 2)
-    totals = loop(second, flux_above(z), (zero,) * 3)
-    kept, found = second(strips, flux_above(z)(strips - 1))
-    totals = tuple(a + b for a, b in zip(totals, found))
-    second(strips + 1, kept)
+    kept, totals = [jnp.zeros((SUB, wide), jnp.float32)] * 2, (zero,) * 3
+    for s in range(strips + 2):
+        kept, found = second(s, kept)
+        totals = tuple(a + b for a, b in zip(totals, found)) if found else totals
 
     def third(s, previous):
         x, y = u[0, at(s), :], u[1, at(s), :]
@@ -311,10 +287,12 @@
         dv = y - below(y, u[1, at(s + 1), :])
         there = eh[1, at(s), :] * (dh * dh) + ev[1, at(s), :] * (dv * dv)
         there = there + y * (given(2, 1, s) * y - exchange)
-        return fv, (folded(x * v + there),)
-
-    (total,) = loop(third, lambda s: down_flux(u, s, 0), (zero,))
-    total = total + third(strips, down_flux(u, strips - 1, 0))[1][0]
+        return fv, folded(x * v + there)
+
+    kept, total = down_flux(u, 0, 0), zero
+    for s in range(1, strips + 1):
+        kept, found = third(s, kept)
+        total = total + found
     lane = lanes_of((1, LANE))
     line = jnp.zeros((1, LANE), jnp.float32)
     for k, value in enumerate(totals + (total,)):
@@ -323,7 +301,8 @@
 
 
 def finish_kernel(parts, fields, z, u, w, v, drop, resid, worst, steps):
-    rows, part = z.shape[0], drop.shape[1]
+    rows, width = w.shape
+    part = drop.shape[1]
 
     @pl.when(pl.program_id(0) == 0)
     def _():
@@ -342,8 +321,9 @@
 
     step, both, mixed = (steps[k, :1, :1] for k in range(3))
     at = pl.ds(pl.multiple_of(pl.program_id(0) * part, SUB), part)
-    here = z[at, :]
-    second_drop = both * here - mixed * u[at, :]
+    inner = pl.ds(pl.multiple_of(2 * SUB + pl.program_id(0) * part, SUB), part)
+    here = z[0, inner, :width]
+    second_drop = both * here - mixed * u[0, inner, :width]
     drop[0] = second_drop
     worst[0] = jnp.maximum(step * here, second_drop)
     given = fields[pl.ds(pl.multiple_of(rows + pl.program_id(0) * part, SUB), part), :]
@@ -409,21 +389,24 @@
     recv = lax.all_to_all(send, ("col", "layer"), 0, 0, tiled=True)
 
     wide = width + LANE
-    pair = pltpu.VMEM((2, rows + 4 * SUB, wide), f32)
+    pair = kept(2, rows + 4 * SUB, wide)
     z, u, w, v, sums = pl.pallas_call(
         grid_kernel,
         in_specs=[vmem] * 4,
         out_specs=[vmem] * 5,
-        out_shape=[kept(rows, width)] * 4 + [kept(n_row * n_col, 1, LANE)],
+        out_shape=[pair] * 2 + [kept(rows, width)] * 2 + [kept(n_row * n_col, 1, LANE)],
         scratch_shapes=[
             pltpu.VMEM((7, rows, LANE), f32),
             pltpu.VMEM((7, 2, SUB, wide), f32),
         ]
-        + [pair] * 6,
+        + [pair] * 4,
         compiler_params=room(28),
         name="grid",
     )(here(bulk), here(other), here(coup), here(recv))
-    parts = lax.all_to_all(sums, ("row", "col"), 0, 0, tiled=True)
+    heart = 3 * n_row // 4
+    order = [heart] + [i for i in range(n_row) if i != heart]
+    group = [i * n_col + k for i in order for k in range(n_col)]
+    parts = lax.all_to_all(sums, ("row", "col"), 0, 0, axis_index_groups=[group], tiled=True)
 
     pieces = 2
     deep = pl.BlockSpec((1, rows // pieces, width), lambda i: (0, i, 0))

time: 104 us -> 100 us (0.962)
  the two profiles are of different devices: /device:TPU:40 before, /device:TPU:33 now
where the time goes in v5:
time: 100 us; the launch traced here: 98.3 us
  starting transfers between devices  46.1 us (46%)
  blocking collectives  41.2 us (41%)
  Pallas kernels  7.18 us (7%)
  waiting for transfers between devices  3.11 us (3%)
    ppermute x1, starting transfers between devices, local(): other = lax.ppermute(bulk, 'layer', swap)  39.5 us
    all_to_all x1, blocking collectives, local(): lax.all_to_all(sums, ('row', 'col'), 0, 0, axis_index_groups=[group], til...  33.9 us
    all_to_all x1, blocking collectives, local(): recv = lax.all_to_all(send, ('col', 'layer'), 0, 0, tiled=True)  7.29 us
    ppermute x1, starting transfers between devices, local(): top = lax.ppermute(down, 'row', up_pairs)  5.25 us
    pallas_call x1, Pallas kernels, local(): pl.pallas_call(grid_kernel, in_specs=[vmem] * 4, out_specs=[vmem] * 5, ou...  3.21 us
    ppermute x1, waiting for transfers between devices, local(): bottom = lax.ppermute(up, 'row', down_pairs)  3.1 us
  transfers between devices with their start and end apart: 3, of which 1 were waited for; matrix products, arithmetic and copies ran while one was open for 0% of the time, Pallas kernels for 1%

profile of v5, /device:TPU:33, one launch (start us, length us, event | category | flops | bytes accessed | tf_op | source)
XLA Modules:
  0.0 98.3 jit_solution(6795250984226745406)
XLA Ops:
  0.6 0.0 copy-start.3
  0.6 0.0 copy-start.2
  0.7 0.0 copy-start.4
  0.7 0.0 copy-start
  0.7 0.0 copy-start.1
  0.7 1.1 %border_rows.1 = (f32[8,1024]{1,0:T(8,128)S(1)}, f32[8,1024]{1,0:T(8,128)S(1)}) custom-call(f32[1,8]{1,0:T(1,128)} %table.3, s32[1,128,1024]{2,1,0:T(8,128)} %cb.1, f32[1,128,1024]{2,1,0:T(8,128)} %rb.1, s32[1,128,1024]{2,1,0:T(8,128)} %pb.1, s32[128,1024]{1,0:T(8,128)} %vb.1, s32[1,128,1024]{2,1,0:T(8,128)} %cb.1, f32[1,128,1024]{2,1,0:T(8,128)} %rb.1, ...), custom_call_target="tpu_custom_call" | custom-call | tf_op jit(solution)/shard_map/border_rows/pallas_call | solution.py:358
  1.8 5.3 %collective-permute-start = (f32[8,1024]{1,0:T(8,128)S(1)}, f32[8,1024]{1,0:T(8,128)S(1)}, u32[]{:S(2)}, u32[]{:S(2)}) collective-permute-start(f32[8,1024]{1,0:T(8,128)S(1)} %get-tuple-element.14), channel_id=1, source_target_pairs={{0,8},{8,16},{16,24},{24,32},{32,40},{40,48},{48,56},{56,64},{64,7... | collective-permute-start | bytes 98312 | tf_op jit(solution)/shard_map/ppermute | solution.py:367
  7.0 1.3 %collective-permute-start.1 = (f32[8,1024]{1,0:T(8,128)S(1)}, f32[8,1024]{1,0:T(8,128)S(1)}, u32[]{:S(2)}, u32[]{:S(2)}) collective-permute-start(f32[8,1024]{1,0:T(8,128)S(1)} %get-tuple-element.15), channel_id=1, source_target_pairs={{8,0},{16,8},{24,16},{32,24},{40,32},{48,40},{56,48},{64,56},{72,6... | collective-permute-start | bytes 98312 | tf_op jit(solution)/shard_map/ppermute | solution.py:368
  8.4 0.0 copy-done.3
  8.4 0.0 copy-done.2
  8.4 0.0 copy-done.4
  8.4 0.0 copy-done
  8.4 0.0 copy-done.1
  8.4 1.3 %tile_fields.1 = (f32[400,1024]{1,0:T(8,128)S(1)}, f32[128,1024]{1,0:T(8,128)S(1)}, f32[16,128]{1,0:T(8,128)S(1)}) custom-call(f32[1,8]{1,0:T(1,128)S(1)} %copy-done.4, s32[1,128,1024]{2,1,0:T(8,128)S(1)} %copy-done, f32[1,128,1024]{2,1,0:T(8,128)S(1)} %copy-done.1, s32[1,128,1024]{2,1,0:T(8,128)S(1)} %copy-done.2, s32[128,1024]{1,0:T(8,128)S(1)} %copy-done.3), custom_call_target="tpu_custom_call" | custom-call | tf_op jit(solution)/shard_map/tile_fields/pallas_call | solution.py:370
  9.7 0.0 collective-permute-done.top
  9.7 3.1 %collective-permute-done.1.bottom = f32[8,1024]{1,0:T(8,128)S(1)} collective-permute-done((f32[8,1024]{1,0:T(8,128)S(1)}, f32[8,1024]{1,0:T(8,128)S(1)}, u32[]{:S(2)}, u32[]{:S(2)}) %collective-permute-start.1) | collective-permute-done | bytes 32800 | tf_op jit(solution)/shard_map/ppermute | solution.py:368
  12.8 39.5 %collective-permute-start.2 = (f32[400,1024]{1,0:T(8,128)S(1)}, f32[400,1024]{1,0:T(8,128)S(1)}, u32[]{:S(2)}, u32[]{:S(2)}) collective-permute-start(f32[400,1024]{1,0:T(8,128)S(1)} %constant_dynamic-update-slice_fusion.own.fields), channel_id=1, source_target_pairs={{0,1},{1,0},{2,3},{3,2},{4,5},{5,4},{6,7},{7,6},{8,9},{9,8},{10,11... | collective-permute-start | bytes 4915208 | tf_op jit(solution)/shard_map/ppermute | solution.py:388
  52.3 0.2 border_columns.1
  52.5 7.3 %all_to_all.10.recv = f32[8,8,256]{2,1,0:T(8,128)S(1)} all-to-all(f32[8,8,256]{2,1,0:T(8,128)S(1)} %border_columns.1), channel_id=1, replica_groups=mesh['scen'=2,'row'=32,'col'=4,'layer'=2] {'col','layer'}, dimensions={0} | all-to-all | bytes 131072 | tf_op jit(solution)/shard_map/all_to_all | solution.py:389
  59.7 0.0 collective-permute-done.2.other
  59.7 3.2 %grid.1 = (f32[2,160,1152]{2,1,0:T(8,128)S(1)}, f32[2,160,1152]{2,1,0:T(8,128)S(1)}, f32[128,1024]{1,0:T(8,128)S(1)}, f32[128,1024]{1,0:T(8,128)S(1)}, f32[128,1,128]{2,1,0:T(1,128)S(1)}) custom-call(f32[400,1024]{1,0:T(8,128)S(1)} %constant_dynamic-update-slice_fusion.own.fields, f32[400,1024]{1,0:T(8,128)S(1)} %collective-permute-done.2.other, ...), custom_call_target="tpu_custom_call" | custom-call | tf_op jit(solution)/shard_map/grid/pallas_call | solution.py:393
  63.0 33.9 %all_to_all.11.parts = f32[128,1,128]{2,1,0:T(1,128)S(1)} all-to-all(f32[128,1,128]{2,1,0:T(1,128)S(1)} %get-tuple-element.18), channel_id=1, replica_groups={{192,194,196,198,0,2,4,6,8,10,12,14,16,18,20,22,24,26,28,30,32,34,36,38..., dimensions={0} | all-to-all | bytes 131072 | tf_op jit(solution)/shard_map/all_to_all | solution.py:409
  96.8 1.5 %finish.1 = (f32[1,128,1024]{2,1,0:T(8,128)}, f32[1,128,1024]{2,1,0:T(8,128)}, f32[1,128,1024]{2,1,0:T(8,128)}) custom-call(f32[128,1,128]{2,1,0:T(1,128)S(1)} %all_to_all.11.parts, f32[400,1024]{1,0:T(8,128)S(1)} %constant_dynamic-update-slice_fusion.own.fields, f32[2,160,1152]{2,1,0:T(8,128)S(1)} %get-tuple-element.19.z, ...), custom_call_target="tpu_custom_call" | custom-call | tf_op jit(solution)/shard_map/finish/pallas_call | solution.py:413
  (2 shorter events, 0.0 us)
Async XLA Ops:
  0.6 7.7 %copy-start.3 = (s32[128,1024]{1,0:T(8,128)S(1)}, s32[128,1024]{1,0:T(8,128)}, u32[]{:S(2)}) copy-start(s32[128,1024]{1,0:T(8,128)} %vb.1) | copy-start | bytes 1572868
  0.6 7.7 %copy-start.2 = (s32[1,128,1024]{2,1,0:T(8,128)S(1)}, s32[1,128,1024]{2,1,0:T(8,128)}, u32[]{:S(2)}) copy-start(s32[1,128,1024]{2,1,0:T(8,128)} %pb.1) | copy-start | bytes 1572868
  0.7 7.7 %copy-start.4 = (f32[1,8]{1,0:T(1,128)S(1)}, f32[1,8]{1,0:T(1,128)}, u32[]{:S(2)}) copy-start(f32[1,8]{1,0:T(1,128)} %table.3) | copy-start | bytes 100
  0.7 7.7 %copy-start = (s32[1,128,1024]{2,1,0:T(8,128)S(1)}, s32[1,128,1024]{2,1,0:T(8,128)}, u32[]{:S(2)}) copy-start(s32[1,128,1024]{2,1,0:T(8,128)} %cb.1) | copy-start | bytes 1572868
  0.7 7.7 %copy-start.1 = (f32[1,128,1024]{2,1,0:T(8,128)S(1)}, f32[1,128,1024]{2,1,0:T(8,128)}, u32[]{:S(2)}) copy-start(f32[1,128,1024]{2,1,0:T(8,128)} %rb.1) | copy-start | bytes 1572868
  1.8 7.9 %collective-permute-start = (f32[8,1024]{1,0:T(8,128)S(1)}, f32[8,1024]{1,0:T(8,128)S(1)}, u32[]{:S(2)}, u32[]{:S(2)}) collective-permute-start(f32[8,1024]{1,0:T(8,128)S(1)} %get-tuple-element.14), channel_id=1, source_target_pairs={{0,8},{8,16},{16,24},{24,32},{32,40},{40,48},{48,56},{56,64},{64,7... | collective-permute-start | bytes 98312 | tf_op jit(solution)/shard_map/ppermute | solution.py:367
  7.0 5.7 %collective-permute-start.1 = (f32[8,1024]{1,0:T(8,128)S(1)}, f32[8,1024]{1,0:T(8,128)S(1)}, u32[]{:S(2)}, u32[]{:S(2)}) collective-permute-start(f32[8,1024]{1,0:T(8,128)S(1)} %get-tuple-element.15), channel_id=1, source_target_pairs={{8,0},{16,8},{24,16},{32,24},{40,32},{48,40},{56,48},{64,56},{72,6... | collective-permute-start | bytes 98312 | tf_op jit(solution)/shard_map/ppermute | solution.py:368
  12.8 47.0 %collective-permute-start.2 = (f32[400,1024]{1,0:T(8,128)S(1)}, f32[400,1024]{1,0:T(8,128)S(1)}, u32[]{:S(2)}, u32[]{:S(2)}) collective-permute-start(f32[400,1024]{1,0:T(8,128)S(1)} %constant_dynamic-update-slice_fusion.own.fields), channel_id=1, source_target_pairs={{0,1},{1,0},{2,3},{3,2},{4,5},{5,4},{6,7},{7,6},{8,9},{9,8},{10,11... | collective-permute-start | bytes 4915208 | tf_op jit(solution)/shard_map/ppermute | solution.py:388

commit v6 on v5

--- a/solution.py
+++ b/solution.py
@@ -11,6 +11,7 @@
 leakage = 0.05
 
 SUB = 8
+TURN = 2
 LANE = 128
 
 
@@ -81,15 +82,12 @@
     rows, width = vias.shape
     fields = [bulk.at[pl.ds(k * rows, rows)] for k in range(3)]
 
-    def strip(s, carry):
-        at = pl.ds(pl.multiple_of(s * SUB, SUB), SUB)
+    for s in range(rows // SUB):
+        at = pl.ds(s * SUB, SUB)
         fields[0][at, :] = half_conductance(classes[0, at, :], table)
         fields[1][at, :] = current[0, at, :]
         fields[2][at, :] = pad_term(pads[0, at, :])
         coup[at, :] = via_term(vias[at, :])
-        return carry
-
-    lax.fori_loop(0, rows // SUB, strip, 0)
     sides = [
         tuple(field[:, at] for field in fields) + (coup[:, at],)
         for at in (slice(0, LANE), slice(width - LANE, width))
@@ -119,8 +117,9 @@
     around = jnp.concatenate([around, jnp.zeros((LANE - 2 * SUB, LANE), jnp.float32)], axis=0).T
     high = jnp.concatenate([strips[:SUB], around[:SUB]], axis=1)
     low = jnp.concatenate([strips[SUB:], around[SUB : 2 * SUB]], axis=1)
-    for k in range(send.shape[0]):
-        send[k] = jnp.where(k // 2 > c, high, low)
+    count = send.shape[0] // 2
+    for k in range(2 * count):
+        send[k] = jnp.where((k // 2 + TURN) % count > c, high, low)
 
 
 def side_lanes(left, right, rows=LANE):
@@ -148,9 +147,9 @@
 
     for layer in range(2):
         mine = place if layer == 0 else 1 - place
-        left = recv[jnp.maximum(2 * (c - 1) + mine, 0)]
+        left = recv[2 * lax.rem(c - 1 - TURN + 4 * columns, columns) + mine]
         left = jnp.where(c > 0, left, 0.0)
-        right = recv[jnp.minimum(2 * (c + 1) + mine, 2 * columns - 1)]
+        right = recv[2 * lax.rem(c + 1 - TURN + 4 * columns, columns) + mine]
         right = jnp.where(c < columns - 1, right, 0.0)
         beside = side_lanes(left[:, :LANE], right[:, :LANE])
         corner = side_lanes(left[:, LANE:], right[:, LANE:], 2 * SUB)
@@ -364,8 +363,8 @@
         compiler_params=room(8),
         name="border_rows",
     )(pltpu.with_memory_space_constraint(class_conductance, pltpu.HBM), *far, *far)
+    bottom = lax.ppermute(up, "row", down_pairs)
     top = lax.ppermute(down, "row", up_pairs)
-    bottom = lax.ppermute(up, "row", down_pairs)
 
     bulk, coup, strips = pl.pallas_call(
         tile_kernel,
@@ -386,7 +385,8 @@
         name="border_columns",
     )(here(top), here(bottom), here(strips))
     other = lax.ppermute(bulk, "layer", swap)
-    recv = lax.all_to_all(send, ("col", "layer"), 0, 0, tiled=True)
+    line = [2 * ((i + TURN) % n_col) + k for i in range(n_col) for k in range(2)]
+    recv = lax.all_to_all(send, ("col", "layer"), 0, 0, axis_index_groups=[line], tiled=True)
 
     wide = width + LANE
     pair = kept(2, rows + 4 * SUB, wide)
@@ -403,9 +403,9 @@
         compiler_params=room(28),
         name="grid",
     )(here(bulk), here(other), here(coup), here(recv))
-    heart = 3 * n_row // 4
+    heart = 13 * n_row // 16
     order = [heart] + [i for i in range(n_row) if i != heart]
-    group = [i * n_col + k for i in order for k in range(n_col)]
+    group = [i * n_col + (k + TURN) % n_col for i in order for k in range(n_col)]
     parts = lax.all_to_all(sums, ("row", "col"), 0, 0, axis_index_groups=[group], tiled=True)
 
     pieces = 2

time: 100 us -> 98.1 us (0.981)
  blocking collectives: 41.2 us -> 39.2 us
    all_to_all x1, blocking collectives: 33.9 us -> 32.6 us  [local(): lax.all_to_all(sums, ('row', 'col'), 0, 0, axis_index_groups=[group], til...]
where the time goes in v6:
time: 98.1 us; the launch traced here: 96.3 us
  starting transfers between devices  46.1 us (47%)
  blocking collectives  39.2 us (40%)
  Pallas kernels  6.96 us (7%)
  waiting for transfers between devices  3.31 us (3%)
    ppermute x1, starting transfers between devices, local(): other = lax.ppermute(bulk, 'layer', swap)  39.5 us
    all_to_all x1, blocking collectives, local(): lax.all_to_all(sums, ('row', 'col'), 0, 0, axis_index_groups=[group], til...  32.6 us
    all_to_all x1, blocking collectives, local(): lax.all_to_all(send, ('col', 'layer'), 0, 0, axis_index_groups=[line], ti...  6.6 us
    ppermute x1, starting transfers between devices, local(): top = lax.ppermute(down, 'row', up_pairs)  5.25 us
    ppermute x1, waiting for transfers between devices, local(): bottom = lax.ppermute(up, 'row', down_pairs)  3.3 us
    pallas_call x1, Pallas kernels, local(): pl.pallas_call(grid_kernel, in_specs=[vmem] * 4, out_specs=[vmem] * 5, ou...  3.21 us
  transfers between devices with their start and end apart: 3, of which 1 were waited for; matrix products, arithmetic and copies ran while one was open for 0% of the time, Pallas kernels for 1%

profile of v6, /device:TPU:33, one launch (start us, length us, event | category | flops | bytes accessed | tf_op | source)
XLA Modules:
  0.0 96.3 jit_solution(13224072953303897728)
XLA Ops:
  0.6 0.0 copy-start.3
  0.6 0.0 copy-start.2
  0.7 0.0 copy-start.4
  0.7 0.0 copy-start
  0.7 0.0 copy-start.1
  0.7 1.1 %border_rows.1 = (f32[8,1024]{1,0:T(8,128)S(1)}, f32[8,1024]{1,0:T(8,128)S(1)}) custom-call(f32[1,8]{1,0:T(1,128)} %table.3, s32[1,128,1024]{2,1,0:T(8,128)} %cb.1, f32[1,128,1024]{2,1,0:T(8,128)} %rb.1, s32[1,128,1024]{2,1,0:T(8,128)} %pb.1, s32[128,1024]{1,0:T(8,128)} %vb.1, s32[1,128,1024]{2,1,0:T(8,128)} %cb.1, f32[1,128,1024]{2,1,0:T(8,128)} %rb.1, ...), custom_call_target="tpu_custom_call" | custom-call | tf_op jit(solution)/shard_map/border_rows/pallas_call | solution.py:357
  1.8 5.3 %collective-permute-start = (f32[8,1024]{1,0:T(8,128)S(1)}, f32[8,1024]{1,0:T(8,128)S(1)}, u32[]{:S(2)}, u32[]{:S(2)}) collective-permute-start(f32[8,1024]{1,0:T(8,128)S(1)} %get-tuple-element.14), channel_id=1, source_target_pairs={{0,8},{8,16},{16,24},{24,32},{32,40},{40,48},{48,56},{56,64},{64,7... | collective-permute-start | bytes 98312 | tf_op jit(solution)/shard_map/ppermute | solution.py:367
  7.0 1.3 %collective-permute-start.1 = (f32[8,1024]{1,0:T(8,128)S(1)}, f32[8,1024]{1,0:T(8,128)S(1)}, u32[]{:S(2)}, u32[]{:S(2)}) collective-permute-start(f32[8,1024]{1,0:T(8,128)S(1)} %get-tuple-element.15), channel_id=1, source_target_pairs={{8,0},{16,8},{24,16},{32,24},{40,32},{48,40},{56,48},{64,56},{72,6... | collective-permute-start | bytes 98312 | tf_op jit(solution)/shard_map/ppermute | solution.py:366
  8.4 0.0 copy-done.3
  8.4 0.0 copy-done.2
  8.4 0.0 copy-done.4
  8.4 0.0 copy-done
  8.4 0.0 copy-done.1
  8.4 1.0 %tile_fields.1 = (f32[400,1024]{1,0:T(8,128)S(1)}, f32[128,1024]{1,0:T(8,128)S(1)}, f32[16,128]{1,0:T(8,128)S(1)}) custom-call(f32[1,8]{1,0:T(1,128)S(1)} %copy-done.4, s32[1,128,1024]{2,1,0:T(8,128)S(1)} %copy-done, f32[1,128,1024]{2,1,0:T(8,128)S(1)} %copy-done.1, s32[1,128,1024]{2,1,0:T(8,128)S(1)} %copy-done.2, s32[128,1024]{1,0:T(8,128)S(1)} %copy-done.3), custom_call_target="tpu_custom_call" | custom-call | tf_op jit(solution)/shard_map/tile_fields/pallas_call | solution.py:369
  9.4 0.0 collective-permute-done.top
  9.5 3.3 %collective-permute-done.1.bottom = f32[8,1024]{1,0:T(8,128)S(1)} collective-permute-done((f32[8,1024]{1,0:T(8,128)S(1)}, f32[8,1024]{1,0:T(8,128)S(1)}, u32[]{:S(2)}, u32[]{:S(2)}) %collective-permute-start.1) | collective-permute-done | bytes 32800 | tf_op jit(solution)/shard_map/ppermute | solution.py:366
  12.8 39.5 %collective-permute-start.2 = (f32[400,1024]{1,0:T(8,128)S(1)}, f32[400,1024]{1,0:T(8,128)S(1)}, u32[]{:S(2)}, u32[]{:S(2)}) collective-permute-start(f32[400,1024]{1,0:T(8,128)S(1)} %constant_dynamic-update-slice_fusion.own.fields), channel_id=1, source_target_pairs={{0,1},{1,0},{2,3},{3,2},{4,5},{5,4},{6,7},{7,6},{8,9},{9,8},{10,11... | collective-permute-start | bytes 4915208 | tf_op jit(solution)/shard_map/ppermute | solution.py:387
  52.3 0.2 border_columns.1
  52.5 6.6 %all_to_all.10.recv = f32[8,8,256]{2,1,0:T(8,128)S(1)} all-to-all(f32[8,8,256]{2,1,0:T(8,128)S(1)} %border_columns.1), channel_id=1, replica_groups={{4,5,6,7,0,1,2,3},{12,13,14,15,8,9,10,11},{20,21,22,23,16,17,18,19},{28..., dimensions={0} | all-to-all | bytes 131072 | tf_op jit(solution)/shard_map/all_to_all | solution.py:389
  59.0 0.0 collective-permute-done.2.other
  59.1 3.2 %grid.1 = (f32[2,160,1152]{2,1,0:T(8,128)S(1)}, f32[2,160,1152]{2,1,0:T(8,128)S(1)}, f32[128,1024]{1,0:T(8,128)S(1)}, f32[128,1024]{1,0:T(8,128)S(1)}, f32[128,1,128]{2,1,0:T(1,128)S(1)}) custom-call(f32[400,1024]{1,0:T(8,128)S(1)} %constant_dynamic-update-slice_fusion.own.fields, f32[400,1024]{1,0:T(8,128)S(1)} %collective-permute-done.2.other, ...), custom_call_target="tpu_custom_call" | custom-call | tf_op jit(solution)/shard_map/grid/pallas_call | solution.py:393
  62.3 32.6 %all_to_all.11.parts = f32[128,1,128]{2,1,0:T(1,128)S(1)} all-to-all(f32[128,1,128]{2,1,0:T(1,128)S(1)} %get-tuple-element.18), channel_id=1, replica_groups={{212,214,208,210,4,6,0,2,12,14,8,10,20,22,16,18,28,30,24,26,36,38,32,34..., dimensions={0} | all-to-all | bytes 131072 | tf_op jit(solution)/shard_map/all_to_all | solution.py:409
  94.8 1.5 %finish.1 = (f32[1,128,1024]{2,1,0:T(8,128)}, f32[1,128,1024]{2,1,0:T(8,128)}, f32[1,128,1024]{2,1,0:T(8,128)}) custom-call(f32[128,1,128]{2,1,0:T(1,128)S(1)} %all_to_all.11.parts, f32[400,1024]{1,0:T(8,128)S(1)} %constant_dynamic-update-slice_fusion.own.fields, f32[2,160,1152]{2,1,0:T(8,128)S(1)} %get-tuple-element.19.z, ...), custom_call_target="tpu_custom_call" | custom-call | tf_op jit(solution)/shard_map/finish/pallas_call | solution.py:413
  (2 shorter events, 0.0 us)
Async XLA Ops:
  0.6 7.7 %copy-start.3 = (s32[128,1024]{1,0:T(8,128)S(1)}, s32[128,1024]{1,0:T(8,128)}, u32[]{:S(2)}) copy-start(s32[128,1024]{1,0:T(8,128)} %vb.1) | copy-start | bytes 1572868
  0.6 7.7 %copy-start.2 = (s32[1,128,1024]{2,1,0:T(8,128)S(1)}, s32[1,128,1024]{2,1,0:T(8,128)}, u32[]{:S(2)}) copy-start(s32[1,128,1024]{2,1,0:T(8,128)} %pb.1) | copy-start | bytes 1572868
  0.7 7.7 %copy-start.4 = (f32[1,8]{1,0:T(1,128)S(1)}, f32[1,8]{1,0:T(1,128)}, u32[]{:S(2)}) copy-start(f32[1,8]{1,0:T(1,128)} %table.3) | copy-start | bytes 100
  0.7 7.7 %copy-start = (s32[1,128,1024]{2,1,0:T(8,128)S(1)}, s32[1,128,1024]{2,1,0:T(8,128)}, u32[]{:S(2)}) copy-start(s32[1,128,1024]{2,1,0:T(8,128)} %cb.1) | copy-start | bytes 1572868
  0.7 7.7 %copy-start.1 = (f32[1,128,1024]{2,1,0:T(8,128)S(1)}, f32[1,128,1024]{2,1,0:T(8,128)}, u32[]{:S(2)}) copy-start(f32[1,128,1024]{2,1,0:T(8,128)} %rb.1) | copy-start | bytes 1572868
  1.8 7.7 %collective-permute-start = (f32[8,1024]{1,0:T(8,128)S(1)}, f32[8,1024]{1,0:T(8,128)S(1)}, u32[]{:S(2)}, u32[]{:S(2)}) collective-permute-start(f32[8,1024]{1,0:T(8,128)S(1)} %get-tuple-element.14), channel_id=1, source_target_pairs={{0,8},{8,16},{16,24},{24,32},{32,40},{40,48},{48,56},{56,64},{64,7... | collective-permute-start | bytes 98312 | tf_op jit(solution)/shard_map/ppermute | solution.py:367
  7.0 5.7 %collective-permute-start.1 = (f32[8,1024]{1,0:T(8,128)S(1)}, f32[8,1024]{1,0:T(8,128)S(1)}, u32[]{:S(2)}, u32[]{:S(2)}) collective-permute-start(f32[8,1024]{1,0:T(8,128)S(1)} %get-tuple-element.15), channel_id=1, source_target_pairs={{8,0},{16,8},{24,16},{32,24},{40,32},{48,40},{56,48},{64,56},{72,6... | collective-permute-start | bytes 98312 | tf_op jit(solution)/shard_map/ppermute | solution.py:366
  12.8 46.3 %collective-permute-start.2 = (f32[400,1024]{1,0:T(8,128)S(1)}, f32[400,1024]{1,0:T(8,128)S(1)}, u32[]{:S(2)}, u32[]{:S(2)}) collective-permute-start(f32[400,1024]{1,0:T(8,128)S(1)} %constant_dynamic-update-slice_fusion.own.fields), channel_id=1, source_target_pairs={{0,1},{1,0},{2,3},{3,2},{4,5},{5,4},{6,7},{7,6},{8,9},{9,8},{10,11... | collective-permute-start | bytes 4915208 | tf_op jit(solution)/shard_map/ppermute | solution.py:387
